TPU v7x, 32 devices: a whole 2x2x4 slice. The times are simulated.
32 devices in a mesh: gz: 2 (over x), gx: 4 (over y, core), gy: 4 (over z).
Axes of the slice: x: 2, y: 2, z: 4, core: 2. Of those that a mesh axis runs over, the one named last changes fastest.
Arguments:
- right_side: float32 [16, 3, 32, 1024], P('gz', None, 'gy', 'gx'), may hold values from -6 to 6
- start_field: float32 [16, 3, 32, 1024], P('gz', None, 'gy', 'gx'), may hold values from -6 to 6
- layer_material: int32 [16], P('gz'), may hold values from 0 to 7
- stiffness: float32 [8, 3, 3, 3], replicated, may hold values from -0.2 to 8, as said below
- line_factors: float32 [8, 3, 3, 3], replicated, may hold values from -0.05 to 1
Outputs:
- solution_field: float32 [16, 3, 32, 1024], P('gz', None, 'gy', 'gx')
- final_residual: float32 [16, 3, 32, 1024], P('gz', None, 'gy', 'gx')
Inputs may be any that keep to these rules, and one draw needn't show every extreme that they name: `stiffness`: diagonal blocks dominate each row over the lateral and vertical couplings of the stencil.
All inputs are finite; a program needn't handle non-finite values.
Results may differ from a plain program's by a relative error of at most 0.0001.
Values sent between devices are 32-bit elements; how exact they have to be, the bound alone decides.
A program may use at most 64 MiB of HBM per device.

v0:
```python
import functools

import jax
import jax.numpy as jnp
from jax import lax
from jax.experimental import pallas as pl
from jax.experimental.pallas import tpu as pltpu
from jax.sharding import PartitionSpec as P

SWEEPS = 3
MESH = pl.DeviceIdType.MESH


def total(terms):
    result = terms[0]
    for term in terms[1:]:
        result = result + term
    return result


def kernel(
    sizes, material, sten, fac, load, start, out_u, out_r,
    cor, crhs, res, loc, chain, chainx, hal, chal, below, above, cbelow, cabove,
    row_out, row_in, crow_out, crow_in, col_out, col_in,
    gather, maps, grow_out, grow_in, gcol_out, gcol_in,
    row_ss, row_rs, col_ss, col_rs, z_ss, z_rs, map_ss, map_rs, zh_ss, zh_rs,
    gr_ss, gr_rs, gc_ss, gc_rs,
):
    nz, ny, nx = sizes
    layers, comps, rows, lanes = load.shape
    half = layers // 2
    gz, gy, gx = (lax.axis_index(name) for name in ("gz", "gy", "gx"))
    wide = col_in.shape[-1]
    row_id = lax.broadcasted_iota(jnp.int32, (rows, lanes), 0)
    lane_id = lax.broadcasted_iota(jnp.int32, (rows, lanes), 1)
    col_id = lax.broadcasted_iota(jnp.int32, (rows, wide), 1)
    top, bottom = row_id == 0, row_id == rows - 1
    first, last = lane_id == 0, lane_id == lanes - 1
    three = range(comps)
    pending = []

    def block(table, level, layer, which):
        mat_id = material[layer * (2 if level else 1)]
        scale = 0.25 if level and table is sten and which == 2 else None
        values = [[table[which, i, j, mat_id] for j in three] for i in three]
        if scale is not None:
            values = [[scale * v for v in line] for line in values]
        return values

    def times(mat, vec):
        return [total([mat[i][j] * vec[j] for j in three]) for i in three]

    def at(z, y, x):
        return {"gz": z, "gy": y, "gx": x}

    def copy_if(cond, src, dst, ss, rs, target):
        copy = pltpu.make_async_remote_copy(
            src_ref=src, dst_ref=dst, send_sem=ss, recv_sem=rs,
            device_id=target, device_id_type=MESH,
        )

        @pl.when(cond)
        def _():
            copy.start()

        pending.append((cond, copy))

    def arrive_if(cond, ref, ss, rs):
        @pl.when(cond)
        def _():
            pltpu.make_async_remote_copy(
                src_ref=ref, dst_ref=ref, send_sem=ss, recv_sem=rs,
                device_id=at(gz, gy, gx), device_id_type=MESH,
            ).wait_recv()

    has_prev_y, has_next_y = gy > 0, gy < ny - 1
    has_prev_x, has_next_x = gx > 0, gx < nx - 1
    has_below, has_above = gz > 0, gz < nz - 1

    barrier = pltpu.get_barrier_semaphore()
    peers = [(gz != j, at(j, gy, gx)) for j in range(nz)]
    peers += [(has_prev_y, at(gz, gy - 1, gx)), (has_next_y, at(gz, gy + 1, gx))]
    peers += [(has_prev_x, at(gz, gy, gx - 1)), (has_next_x, at(gz, gy, gx + 1))]
    sides_y = ((has_next_y, gy + 1), (has_prev_y, gy - 1))
    sides_x = ((has_next_x, gx + 1), (has_prev_x, gx - 1))
    for j in range(nz):
        peers += [(jnp.logical_and(gz != j, cond), at(j, spot, gx)) for cond, spot in sides_y]
        peers += [(jnp.logical_and(gz != j, cond), at(j, gy, spot)) for cond, spot in sides_x]
    for cond, target in peers:
        @pl.when(cond)
        def _(target=target):
            pl.semaphore_signal(barrier, inc=1, device_id=target, device_id_type=MESH)

    for side, cond in enumerate((has_prev_y, has_next_y)):
        @pl.when(jnp.logical_not(cond))
        def _(side=side):
            row_in[:, side] = jnp.zeros_like(row_in[:, side])
            crow_in[:, side] = jnp.zeros_like(crow_in[:, side])
            grow_in[:, :, side] = jnp.zeros_like(grow_in[:, :, side])
    for side, cond in enumerate((has_prev_x, has_next_x)):
        @pl.when(jnp.logical_not(cond))
        def _(side=side):
            col_in[:, side] = jnp.zeros_like(col_in[:, side])
            gcol_in[:, :, side] = jnp.zeros_like(gcol_in[:, :, side])
    for cond, ref in ((has_below, below), (has_above, above)):
        @pl.when(jnp.logical_not(cond))
        def _(ref=ref):
            ref[...] = jnp.zeros_like(ref)
    for j in range(nz):
        @pl.when(gz > j)
        def _(j=j):
            gather[:, 1, j] = jnp.zeros_like(gather[:, 1, j])

    row_out[:, :, layers * comps :] = jnp.zeros_like(row_out[:, :, layers * comps :])
    crow_out[:, :, half * comps :] = jnp.zeros_like(crow_out[:, :, half * comps :])
    grow_out[...] = jnp.zeros_like(grow_out)

    corner_id = lax.broadcasted_iota(jnp.int32, (rows, 128), 1)
    basis_lane = lax.broadcasted_iota(jnp.int32, (8, 128), 1)
    basis = [(basis_lane == c).astype(jnp.float32) for c in three]
    for level, count in ((0, layers), (1, half)):
        ups = []
        carry = basis
        for layer in range(count):
            carry = times(block(fac, level, layer, 1), carry)
            ups.append(carry)
        turned, back = None, basis
        for layer in reversed(range(count)):
            mat = block(fac, level, layer, 2)
            turned = ups[layer] if turned is None else [
                a + b for a, b in zip(ups[layer], times(mat, turned))
            ]
            back = times(mat, back)
            if layer == count - 1:
                edge = back
        for kind, value in enumerate((ups[-1], turned, back, edge)):
            for c in three:
                maps[gz, level, kind, c] = value[c]

    def held(level, owner, kind, width):
        tiles = [maps[owner, level, kind, c] for c in three]
        return [[jnp.broadcast_to(tiles[i][:rows, j : j + 1], (rows, width)) for j in three] for i in three]

    def send_sides(phase, level, field, count, tail=None):
        out, into = (crow_out, crow_in) if level else (row_out, row_in)
        slot = phase - SWEEPS - 1 if level else phase
        tiles = [jnp.zeros((rows, wide), jnp.float32)] * 2
        for layer in range(count + (tail is not None)):
            for c in three:
                spot = layer * comps + c
                value = field[layer, c] if layer < count else tail[c]
                out[slot, 0, spot : spot + 1, :] = value[rows - 1 : rows, :]
                out[slot, 1, spot : spot + 1, :] = value[0:1, :]
                here = col_id == spot
                tiles[0] = jnp.where(here, value[:, lanes - 1 : lanes], tiles[0])
                tiles[1] = jnp.where(here, value[:, 0:1], tiles[1])
        for side in range(2):
            col_out[phase, side] = tiles[side]
        for side, cond, target in (
            (0, has_next_y, at(gz, gy + 1, gx)), (1, has_prev_y, at(gz, gy - 1, gx)),
        ):
            copy_if(cond, out.at[slot, side], into.at[slot, side],
                    row_ss.at[phase, side], row_rs.at[phase, side], target)
        for side, cond, target in (
            (0, has_next_x, at(gz, gy, gx + 1)), (1, has_prev_x, at(gz, gy, gx - 1)),
        ):
            copy_if(cond, col_out.at[phase, side], col_in.at[phase, side],
                    col_ss.at[phase, side], col_rs.at[phase, side], target)
        return phase, slot, into

    def await_sides(handle):
        phase, slot, into = handle
        for side, cond in enumerate((has_prev_y, has_next_y)):
            arrive_if(cond, into.at[slot, side], row_ss.at[phase, side], row_rs.at[phase, side])
        for side, cond in enumerate((has_prev_x, has_next_x)):
            arrive_if(cond, col_in.at[phase, side], col_ss.at[phase, side], col_rs.at[phase, side])

    def inner_residual(level, field, source, low, high, count):
        for layer in range(count):
            here = [field[layer, c] for c in three]
            side, vert = [], []
            for c in three:
                x = here[c]
                side.append(
                    (jnp.where(first, 0.0, pltpu.roll(x, 1, 1)) + jnp.where(last, 0.0, pltpu.roll(x, lanes - 1, 1)))
                    + (jnp.where(top, 0.0, pltpu.roll(x, 1, 0)) + jnp.where(bottom, 0.0, pltpu.roll(x, rows - 1, 0)))
                )
                under = field[layer - 1, c] if layer else low[c]
                over = field[layer + 1, c] if layer < count - 1 else high[c]
                vert.append(under + over)
            a = times(block(sten, level, layer, 0), here)
            b = times(block(sten, level, layer, 1), side)
            d = times(block(sten, level, layer, 2), vert)
            for c in three:
                res[layer, c] = source[layer, c] - (a[c] - b[c] - d[c])

    rim_row = jnp.logical_or(top, bottom)
    rim_lane = jnp.logical_or(first, last)

    def full_residual(level, layer):
        rim = chal if level else hal
        edge = [
            jnp.where(rim_row, rim[layer, c][:, :lanes], 0.0) + jnp.where(rim_lane, rim[layer, c][:, lanes:], 0.0)
            for c in three
        ]
        extra = times(block(sten, level, layer, 1), edge)
        return [res[layer, c] + extra[c] for c in three]

    def rim_tile(prev_row, next_row, prev_col, next_col):
        return jnp.concatenate(
            [jnp.where(top, prev_row, next_row), jnp.where(first, prev_col, next_col)], axis=1
        )

    def sides_tile(handle, spot):
        phase, slot, into = handle
        return rim_tile(
            into[slot, 0, spot : spot + 1, :], into[slot, 1, spot : spot + 1, :],
            col_in[phase, 0][:, spot : spot + 1], col_in[phase, 1][:, spot : spot + 1],
        )

    def entry(turn, kind, k, c):
        rim = rim_tile(
            grow_in[turn, kind, 0, k, c : c + 1, :], grow_in[turn, kind, 1, k, c : c + 1, :],
            gcol_in[turn, kind, 0, k][:, c : c + 1], gcol_in[turn, kind, 1, k][:, c : c + 1],
        )
        return gather[turn, kind, k, c], rim

    def send_corners(turn, kind, value, wanted):
        for side, line in ((0, rows - 1), (1, 0)):
            for c in three:
                grow_out[turn, kind, side, c : c + 1, :] = value[c][line : line + 1, :]
        for side, lane in ((0, lanes - 1), (1, 0)):
            tile = jnp.zeros((rows, 128), jnp.float32)
            for c in three:
                tile = jnp.where(corner_id == c, value[c][:, lane : lane + 1], tile)
            gcol_out[turn, kind, side] = tile
        for j in range(nz):
            for side in range(2):
                cond, spot = sides_y[side]
                copy_if(jnp.logical_and(wanted(j), cond), grow_out.at[turn, kind, side],
                        grow_in.at[turn, kind, side, gz],
                        gr_ss.at[turn, kind, side, j], gr_rs.at[turn, kind, side, gz], at(j, spot, gx))
                cond, spot = sides_x[side]
                copy_if(jnp.logical_and(wanted(j), cond), gcol_out.at[turn, kind, side],
                        gcol_in.at[turn, kind, side, gz],
                        gc_ss.at[turn, kind, side, j], gc_rs.at[turn, kind, side, gz], at(j, gy, spot))

    def await_corners(turn, kind, j, wanted):
        for side, (there_y, there_x) in enumerate(((has_prev_y, has_prev_x), (has_next_y, has_next_x))):
            arrive_if(jnp.logical_and(wanted, there_y), grow_in.at[turn, kind, side, j],
                      gr_ss.at[turn, kind, side, j], gr_rs.at[turn, kind, side, j])
            arrive_if(jnp.logical_and(wanted, there_x), gcol_in.at[turn, kind, side, j],
                      gc_ss.at[turn, kind, side, j], gc_rs.at[turn, kind, side, j])

    def line_solve(level, turn, resid, count):
        carry = None
        for layer in range(count):
            now = times(block(fac, level, layer, 0), resid(layer))
            if carry is not None:
                now = [a + b for a, b in zip(now, times(block(fac, level, layer, 1), carry))]
            for c in three:
                chain[layer, c] = now[c]
            carry = now
        for c in three:
            gather[turn, 0, gz, c] = carry[c]
        ending = carry
        if nz > 1:
            send_corners(turn, 0, carry, lambda j: jnp.logical_and(gz != j, gz < nz - 1))
            for j in range(nz):
                copy_if(jnp.logical_and(gz != j, gz < nz - 1), gather.at[turn, 0, gz], gather.at[turn, 0, gz],
                        z_ss.at[turn, 0, j], z_rs.at[turn, 0, gz], at(j, gy, gx))
        back = None
        for layer in reversed(range(count)):
            now = [chain[layer, c] for c in three]
            if back is not None:
                now = [a + b for a, b in zip(now, times(block(fac, level, layer, 2), back))]
            for c in three:
                loc[layer, c] = now[c]
            back = now
        for c in three:
            gather[turn, 1, gz, c] = back[c]
        if nz > 1:
            send_corners(turn, 1, back, lambda j: gz > j)
        for j in range(nz):
            copy_if(gz > j, gather.at[turn, 1, gz], gather.at[turn, 1, gz],
                    z_ss.at[turn, 1, j], z_rs.at[turn, 1, gz], at(j, gy, gx))
        handle = send_sides(turn + 1, level, loc, count, ending)
        for j in range(nz - 1):
            arrive_if(gz != j, gather.at[turn, 0, j], z_ss.at[turn, 0, j], z_rs.at[turn, 0, j])
            await_corners(turn, 0, j, gz != j)
        for j in range(1, nz):
            arrive_if(gz < j, gather.at[turn, 1, j], z_ss.at[turn, 1, j], z_rs.at[turn, 1, j])
            await_corners(turn, 1, j, gz < j)
        await_sides(handle)
        full = 3 * lanes
        zero = [jnp.zeros((rows, full), jnp.float32)] * 3
        ins, outs = [zero], [zero]
        for k in range(nz - 1):
            value = []
            for c in three:
                own, rim = entry(turn, 0, k, c)
                rim = jnp.where(gz == k, sides_tile(handle, count * comps + c), rim)
                value.append(jnp.concatenate([own, rim], axis=1))
            if k:
                value = [a + b for a, b in zip(value, times(held(level, k, 0, full), ins[k]))]
            ins.append(value)
        for k in reversed(range(1, nz)):
            value = [jnp.concatenate(entry(turn, 1, k, c), axis=1) for c in three]
            value = [a + b for a, b in zip(value, times(held(level, k, 1, full), ins[k]))]
            if k < nz - 1:
                value = [a + b for a, b in zip(value, times(held(level, k, 2, full), outs[0]))]
            outs.insert(0, value)
        enter, leave = ins[0], outs[0]
        for k in range(1, nz):
            enter = [jnp.where(gz == k, a, b) for a, b in zip(ins[k], enter)]
            leave = [jnp.where(gz == k, a, b) for a, b in zip(outs[k], leave)]
        carry = enter
        for layer in range(count):
            carry = times(block(fac, level, layer, 1), carry)
            for c in three:
                chainx[layer, c] = carry[c]
        rim, fresh = (chal, turn == SWEEPS) if level else (hal, False)
        carry = leave
        for layer in reversed(range(count)):
            carry = [chainx[layer, c] + b for c, b in enumerate(times(block(fac, level, layer, 2), carry))]
            for c in three:
                loc[layer, c] = loc[layer, c] + carry[c][:, :lanes]
                step = sides_tile(handle, layer * comps + c) + carry[c][:, lanes:]
                rim[layer, c] = step if fresh else rim[layer, c] + step
        under = times(held(level, jnp.maximum(gz - 1, 0), 3, lanes), [loc[0, c] for c in three])
        under = [jnp.where(has_below, enter[c][:, :lanes] + under[c], 0.0) for c in three]
        return under, [leave[c][:, :lanes] for c in three]

    pl.semaphore_wait(barrier, total([cond.astype(jnp.int32) for cond, _ in peers]))

    handle = send_sides(0, 0, start, layers)
    copy_if(has_above, start.at[layers - 1], below, zh_ss.at[0], zh_rs.at[0], at(gz + 1, gy, gx))
    copy_if(has_below, start.at[0], above, zh_ss.at[1], zh_rs.at[1], at(gz - 1, gy, gx))
    for j in range(nz):
        copy_if(gz != j, maps.at[gz], maps.at[gz], map_ss.at[j], map_rs.at[gz], at(j, gy, gx))
    arrive_if(has_below, below, zh_ss.at[0], zh_rs.at[0])
    arrive_if(has_above, above, zh_ss.at[1], zh_rs.at[1])
    for sweep in range(SWEEPS + 1):
        field = out_u if sweep else start
        inner_residual(0, field, load, below, above, layers)
        if sweep == SWEEPS:
            break
        if sweep == 0:
            await_sides(handle)
            for layer in range(layers):
                for c in three:
                    hal[layer, c] = sides_tile(handle, layer * comps + c)
            for j in range(nz):
                arrive_if(gz != j, maps.at[j], map_ss.at[j], map_rs.at[j])
        under, over = line_solve(0, sweep, functools.partial(full_residual, 0), layers)
        for layer in range(layers):
            for c in three:
                out_u[layer, c] = field[layer, c] + loc[layer, c]
        for c in three:
            below[c] = below[c] + under[c]
            above[c] = above[c] + over[c]

    for k in range(half):
        pair = [full_residual(0, 2 * k + step) for step in range(2)]
        for c in three:
            crhs[k, c] = pair[0][c] + pair[1][c]
    for sweep in range(SWEEPS):
        if sweep:
            inner_residual(1, cor, crhs, cbelow, cabove, half)
            source = functools.partial(full_residual, 1)
        else:
            def source(layer):
                return [crhs[layer, c] for c in three]
        under, over = line_solve(1, SWEEPS + sweep, source, half)
        for layer in range(half):
            for c in three:
                value = loc[layer, c]
                cor[layer, c] = cor[layer, c] + value if sweep else value
        for c in three:
            cbelow[c] = cbelow[c] + under[c] if sweep else under[c]
            cabove[c] = cabove[c] + over[c] if sweep else over[c]
    for layer in range(layers):
        for c in three:
            out_u[layer, c] = out_u[layer, c] + cor[layer // 2, c]
            hal[layer, c] = hal[layer, c] + chal[layer // 2, c]
    for c in three:
        below[c] = below[c] + cbelow[c]
        above[c] = above[c] + cabove[c]
    inner_residual(0, out_u, load, below, above, layers)
    for layer in range(layers):
        value = full_residual(0, layer)
        for c in three:
            out_r[layer, c] = value[c]
    for cond, copy in pending:
        @pl.when(cond)
        def _(copy=copy):
            copy.wait_send()


def solution(mesh):
    sizes = tuple(mesh.shape[name] for name in ("gz", "gy", "gx"))
    nz = sizes[0]

    def on_device(right_side, start_field, layer_material, stiffness, line_factors):
        layers, comps, rows, lanes = right_side.shape
        half = layers // 2
        wide = -(-(layers + 1) * comps // 128) * 128
        tall, ctall = (-(-(n + 1) * comps // 8) * 8 for n in (layers, half))
        phases = 2 * SWEEPS + 1
        f32 = jnp.float32
        vmem = pl.BlockSpec(memory_space=pltpu.VMEM)
        smem = pl.BlockSpec(memory_space=pltpu.SMEM)
        dma = pltpu.SemaphoreType.DMA
        scratch = [
            pltpu.VMEM((half, comps, rows, lanes), f32),
            pltpu.VMEM((half, comps, rows, lanes), f32),
            pltpu.VMEM((layers, comps, rows, lanes), f32),
            pltpu.VMEM((layers, comps, rows, lanes), f32),
            pltpu.VMEM((layers, comps, rows, lanes), f32),
            pltpu.VMEM((layers, comps, rows, 3 * lanes), f32),
            pltpu.VMEM((layers, comps, rows, 2 * lanes), f32),
            pltpu.VMEM((half, comps, rows, 2 * lanes), f32),
        ]
        scratch += [pltpu.VMEM((comps, rows, lanes), f32)] * 4
        scratch += [pltpu.VMEM((SWEEPS + 1, 2, tall, lanes), f32)] * 2
        scratch += [pltpu.VMEM((SWEEPS, 2, ctall, lanes), f32)] * 2
        scratch += [pltpu.VMEM((phases, 2, rows, wide), f32)] * 2
        scratch += [
            pltpu.VMEM((2 * SWEEPS, 2, nz, comps, rows, lanes), f32),
            pltpu.VMEM((nz, 2, 4, comps, 8, 128), f32),
            pltpu.VMEM((2 * SWEEPS, 2, 2, 8, lanes), f32),
            pltpu.VMEM((2 * SWEEPS, 2, 2, nz, 8, lanes), f32),
            pltpu.VMEM((2 * SWEEPS, 2, 2, rows, 128), f32),
            pltpu.VMEM((2 * SWEEPS, 2, 2, nz, rows, 128), f32),
        ]
        scratch += [dma((phases, 2))] * 4 + [dma((2 * SWEEPS, 2, nz))] * 2
        scratch += [dma((nz,))] * 2 + [dma((2,))] * 2
        scratch += [dma((2 * SWEEPS, 2, 2, nz))] * 4
        out = jax.ShapeDtypeStruct(right_side.shape, f32)
        return pl.pallas_call(
            functools.partial(kernel, sizes),
            out_shape=(out, out),
            in_specs=[smem, smem, smem, vmem, vmem],
            out_specs=(vmem, vmem),
            scratch_shapes=scratch,
            compiler_params=pltpu.CompilerParams(collective_id=0, has_side_effects=True),
        )(layer_material, stiffness.transpose(1, 2, 3, 0), line_factors.transpose(1, 2, 3, 0), right_side, start_field)

    return jax.shard_map(
        on_device,
        mesh=mesh,
        in_specs=(P("gz", None, "gy", "gx"), P("gz", None, "gy", "gx"), P("gz"), P(), P()),
        out_specs=(P("gz", None, "gy", "gx"), P("gz", None, "gy", "gx")),
        check_vma=False,
    )
```

profile of v0, /device:TPU:1, one launch (start us, length us, event | category | flops | bytes accessed | tf_op | source)
XLA Modules:
  0.0 41.1 jit_solution(17405745817516642027)
XLA Ops:
  0.6 38.2 %shard_map.68 = (f32[8,3,8,256]{3,2,1,0:T(8,128)}, f32[8,3,8,256]{3,2,1,0:T(8,128)}) custom-call(s32[8]{0:T(128)} %material.1, f32[3,3,3,8]{3,2,1,0:T(4,128)} %bitcast.2, f32[3,3,3,8]{3,2,1,0:T(4,128)} %bitcast.3, f32[8,3,8,256]{3,2,1,0:T(8,128)} %load.1, f32[8,3,8,256]{3,2,1,0:T(8,128)} %start.1), custom_call_target="tpu_custom_call" | custom-call | tf_op jit(solution)/shard_map/pallas_call | solution.py:440
  38.8 0.0 copy-start
  38.8 1.7 %copy.9 = f32[8,3,8,256]{3,2,1,0:T(8,128)} copy(f32[8,3,8,256]{3,2,1,0:T(8,128)} %get-tuple-element.4) | data formatting | bytes 393216
  40.5 0.0 copy-done
  40.5 0.7 %copy.10 = f32[8,3,8,256]{3,2,1,0:T(8,128)} copy(f32[8,3,8,256]{3,2,1,0:T(8,128)S(1)} %copy-done) | data formatting | bytes 393216
Async XLA Ops:
  38.8 1.7 %copy-start = (f32[8,3,8,256]{3,2,1,0:T(8,128)S(1)}, f32[8,3,8,256]{3,2,1,0:T(8,128)}, u32[]{:S(2)}) copy-start(f32[8,3,8,256]{3,2,1,0:T(8,128)} %get-tuple-element.5) | copy-start | bytes 589828
where the time goes:
time: 41.7 us; the launch traced here: 41.1 us
  Pallas kernels  38.2 us (92%)
  local copies, waits for them, and re-layouts  2.34 us (6%)
  between operations  0.65 us (2%)
    pallas_call x1, Pallas kernels, on_device(): pl.pallas_call(functools.partial(kernel, sizes), out_shape=(out, out), in...  38.2 us
    unnamed x4, local copies, waits for them, and re-layouts  2.34 us

commit v1 on v0

v1 whole, which is shorter than its diff:
```python
import functools

import jax
import jax.numpy as jnp
from jax import lax
from jax.experimental import pallas as pl
from jax.experimental.pallas import tpu as pltpu
from jax.sharding import PartitionSpec as P

SWEEPS = 3
REACH = 2 * SWEEPS + 1
POWERS = REACH + 1
SLOT = 8
MESH = pl.DeviceIdType.MESH


def total(terms):
    result = terms[0]
    for term in terms[1:]:
        result = result + term
    return result


def kernel(
    sizes, dims, material, sten, fac, load, start, out_u, out_r,
    mats, own_u, own_b, prev_u, prev_b, next_u, next_b, edge_out, edge_in, work, keep,
    sym_u, sym_b, sym_r, sym_y, sym_e, sym_c, maps, left, right, mine, outgoing, incoming,
    mat_ss, mat_rs, row_ss, row_rs, edge_ss, edge_rs, part_ss, part_rs,
):
    nz, ny, nx = sizes
    layers, comps, rows, lanes = dims
    planes = layers * comps
    deep = nz * layers
    width = lanes + 128
    gz, gy, gx = (lax.axis_index(name) for name in ("gz", "gy", "gx"))
    three = range(comps)
    group = right.shape[1] // POWERS
    half_group = group // 2
    pending = []

    def at(z, y, x):
        return {"gz": z, "gy": y, "gx": x}

    def copy_if(cond, src, dst, ss, rs, target):
        copy = pltpu.make_async_remote_copy(
            src_ref=src, dst_ref=dst, send_sem=ss, recv_sem=rs,
            device_id=target, device_id_type=MESH,
        )

        @pl.when(cond)
        def _():
            copy.start()

        pending.append((cond, copy))

    def arrive_if(cond, ref, ss, rs):
        @pl.when(cond)
        def _():
            pltpu.make_async_remote_copy(
                src_ref=ref, dst_ref=ref, send_sem=ss, recv_sem=rs,
                device_id=at(gz, gy, gx), device_id_type=MESH,
            ).wait_recv()

    has_prev_y, has_next_y = gy > 0, gy < ny - 1
    has_prev_x, has_next_x = gx > 0, gx < nx - 1
    sides_y = ((-1, has_prev_y), (0, True), (1, has_next_y))
    sides_x = ((-1, has_prev_x), (1, has_next_x))

    barrier = pltpu.get_barrier_semaphore()
    peers = [(gz != j, at(j, gy, gx)) for j in range(nz)]
    peers += [(cond, at(gz, gy + step, gx)) for step, cond in sides_y if step]
    for step_y, cond_y in sides_y:
        for step_x, cond_x in sides_x:
            peers.append((jnp.logical_and(cond_y, cond_x), at(gz, gy + step_y, gx + step_x)))
    for cond, target in peers:
        @pl.when(cond)
        def _(target=target):
            pl.semaphore_signal(barrier, inc=1, device_id=target, device_id_type=MESH)

    tiles = lanes // 128
    for own, given in ((own_u, start), (own_b, load)):
        for y in range(rows):
            for tile in range(tiles):
                own[y, :, tile * 128 : (tile + 1) * 128] = given[pl.ds(tile * rows + y, planes, stride=tiles * rows), :]

    def place(index):
        return (index * SLOT // 128) * 128, index * SLOT % 128

    tile_lane = lax.broadcasted_iota(jnp.int32, (planes, 128), 1)
    for side in range(2):
        for tile in range(edge_out.shape[2] // 128):
            packed = jnp.zeros((planes, 128), jnp.float32)
            for which, ref in enumerate((own_u, own_b)):
                for y in range(rows):
                    base, spot = place(which * rows + y)
                    if base != tile * 128:
                        continue
                    if side == 0:
                        piece = pltpu.roll(ref[y, :, 0:128], spot, 1) if spot else ref[y, :, 0:128]
                    else:
                        piece = pltpu.roll(ref[y, :, lanes - 128 : lanes], (spot + SLOT) % 128, 1)
                    inside = jnp.logical_and(tile_lane >= spot, tile_lane < spot + SLOT)
                    packed = jnp.where(inside, piece, packed)
            edge_out[side, :, tile * 128 : (tile + 1) * 128] = packed

    pl.semaphore_wait(barrier, total([cond.astype(jnp.int32) for cond, _ in peers]))

    for j in range(nz):
        copy_if(gz != j, material, mats.at[gz], mat_ss.at[j], mat_rs.at[gz], at(j, gy, gx))
    for step_y, cond_y in sides_y:
        for side, (step_x, cond_x) in enumerate(sides_x):
            slot = edge_in.at[1 - side, 1 - step_y]
            copy_if(jnp.logical_and(cond_y, cond_x), edge_out.at[side], slot,
                    edge_ss.at[1 - side, 1 - step_y], edge_rs.at[1 - side, 1 - step_y],
                    at(gz, gy + step_y, gx + step_x))
    strips = ((own_u, prev_u, next_u, REACH), (own_b, prev_b, next_b, REACH - 1))
    for which, (own, prev, after, depth) in enumerate(strips):
        copy_if(has_next_y, own.at[rows - depth : rows], prev,
                row_ss.at[which, 0], row_rs.at[which, 0], at(gz, gy + 1, gx))
        copy_if(has_prev_y, own.at[0:depth], after,
                row_ss.at[which, 1], row_rs.at[which, 1], at(gz, gy - 1, gx))

    for layer in range(layers):
        mats[gz, layer] = material[layer]
    for cond, refs in ((has_prev_y, (prev_u, prev_b)), (has_next_y, (next_u, next_b))):
        @pl.when(jnp.logical_not(cond))
        def _(refs=refs):
            for ref in refs:
                ref[...] = jnp.zeros_like(ref)
    for step_y, cond_y in sides_y:
        for side, (step_x, cond_x) in enumerate(sides_x):
            @pl.when(jnp.logical_not(jnp.logical_and(cond_y, cond_x)))
            def _(side=side, step_y=step_y):
                edge_in[side, 1 + step_y] = jnp.zeros_like(edge_in[side, 1 + step_y])
    wide_lane = lax.broadcasted_iota(jnp.int32, (planes, width), 1)
    inner = (wide_lane < lanes).astype(jnp.float32)
    inner = inner + jnp.where(
        jnp.logical_and(wide_lane >= lanes, wide_lane < lanes + SLOT), has_next_x.astype(jnp.float32), 0.0)
    inner = inner + jnp.where(wide_lane >= width - SLOT, has_prev_x.astype(jnp.float32), 0.0)
    keep[0] = inner * has_prev_y.astype(jnp.float32)
    keep[1] = inner
    keep[2] = inner * has_next_y.astype(jnp.float32)
    for y in range(rows):
        for power in range(POWERS):
            for part in range(2):
                if power == REACH and part == 1:
                    low = 0
                else:
                    low = planes
                if low < half_group:
                    first = power * group + part * half_group + low
                    stop = power * group + (part + 1) * half_group
                    right[y, first:stop, :] = jnp.zeros((stop - first, lanes), jnp.float32)

    sub = lax.broadcasted_iota(jnp.int32, (8, 128), 0)
    lane = lax.broadcasted_iota(jnp.int32, (8, 128), 1)
    lowest = sub == 0

    def block(table, level, layer, which):
        z = layer * (2 if level else 1)
        mat_id = mats[z // layers, z % layers]
        values = [[table[which, i, j, mat_id] for j in three] for i in three]
        if level and table is sten and which == 2:
            values = [[0.25 * v for v in line] for line in values]
        return values

    def times(mat, vec):
        return [total([mat[i][j] * vec[j] for j in three]) for i in three]

    def spread(x):
        return jnp.where(lowest, 0.0, pltpu.roll(x, 1, 0))

    for z in range(deep):
        here = gz == z // layers
        for c in three:
            plane = z % layers * comps + c
            spot = jnp.where(here, plane, -1 - half_group)
            sym_u[z * comps + c] = jnp.logical_and(lowest, lane == spot).astype(jnp.float32)
            sym_b[z * comps + c] = jnp.logical_and(lowest, lane == spot + half_group).astype(jnp.float32)

    def residual(level, field, source, count, layer):
        here = [field[layer * comps + c] for c in three]
        side = [spread(x) for x in here]
        vert = []
        for c in three:
            near = []
            if layer:
                near.append(field[(layer - 1) * comps + c])
            if layer < count - 1:
                near.append(field[(layer + 1) * comps + c])
            vert.append(total(near))
        a = times(block(sten, level, layer, 0), here)
        b = times(block(sten, level, layer, 1), side)
        d = times(block(sten, level, layer, 2), vert)
        return [source[layer * comps + c] - (a[c] - b[c] - d[c]) for c in three]

    def line_solve(level, resid, field, count, fresh):
        carry = None
        for layer in range(count):
            now = times(block(fac, level, layer, 0), resid(layer))
            if carry is not None:
                now = [a + b for a, b in zip(now, times(block(fac, level, layer, 1), carry))]
            for c in three:
                sym_y[layer * comps + c] = now[c]
            carry = now
        back = None
        for layer in reversed(range(count)):
            now = [sym_y[layer * comps + c] for c in three]
            if back is not None:
                now = [a + b for a, b in zip(now, times(block(fac, level, layer, 2), back))]
            for c in three:
                spot = layer * comps + c
                field[spot] = now[c] if fresh else field[spot] + now[c]
            back = now

    for j in range(nz):
        arrive_if(gz != j, mats.at[j], mat_ss.at[j], mat_rs.at[j])
    for sweep in range(SWEEPS):
        line_solve(0, lambda layer: residual(0, sym_u, sym_b, deep, layer), sym_u, deep, False)
    for k in range(deep // 2):
        pair = [residual(0, sym_u, sym_b, deep, 2 * k + step) for step in range(2)]
        for c in three:
            sym_c[k * comps + c] = pair[0][c] + pair[1][c]
    for sweep in range(SWEEPS):
        if sweep:
            source = functools.partial(residual, 1, sym_e, sym_c, deep // 2)
        else:
            def source(layer):
                return [sym_c[layer * comps + c] for c in three]
        line_solve(1, source, sym_e, deep // 2, sweep == 0)
    for z in range(deep):
        for c in three:
            sym_u[z * comps + c] = sym_u[z * comps + c] + sym_e[z // 2 * comps + c]
    for z in range(deep):
        value = residual(0, sym_u, sym_b, deep, z)
        first = z // layers * 2 * planes + z % layers * comps
        for c in three:
            maps[(first + c) * 8 : (first + c + 1) * 8, :] = sym_u[z * comps + c]
            spot = first + planes + c
            maps[spot * 8 : (spot + 1) * 8, :] = value[c]
    for i in range(nz):
        target = lax.rem(gz + 1 + i, nz)
        for pair in range(POWERS * group // 128):
            tile = None
            for part in range(128 // group):
                power = pair * (128 // group) + part
                value = maps[pl.ds(target * 2 * planes * 8 + power, 2 * planes, stride=8), :]
                if part:
                    value = pltpu.roll(value, part * group, 1)
                tile = value if tile is None else tile + value
            left[i * 2 * planes : (i + 1) * 2 * planes, pair * 128 : (pair + 1) * 128] = tile

    for step_y, cond_y in sides_y:
        for side, (step_x, cond_x) in enumerate(sides_x):
            arrive_if(jnp.logical_and(cond_y, cond_x), edge_in.at[side, 1 + step_y],
                      edge_ss.at[side, 1 + step_y], edge_rs.at[side, 1 + step_y])

    def powers(which):
        own, prev, after, depth = strips[which]
        arrive_if(has_prev_y, prev, row_ss.at[which, 0], row_rs.at[which, 0])
        arrive_if(has_next_y, after, row_ss.at[which, 1], row_rs.at[which, 1])

        def raw(y):
            if y < 0:
                middle, step_y, line = prev[depth + y], -1, rows + y
            elif y < rows:
                middle, step_y, line = own[y], 0, y
            else:
                middle, step_y, line = after[y - rows], 1, y - rows
            base, spot = place(which * rows + line)
            west = pltpu.roll(edge_in[0, 1 + step_y, :, base : base + 128], (128 - SLOT - spot) % 128, 1)
            east = edge_in[1, 1 + step_y, :, base : base + 128]
            if spot:
                east = pltpu.roll(east, 128 - spot, 1)
            tail = jnp.where(tile_lane < SLOT, east, jnp.where(tile_lane >= 128 - SLOT, west, 0.0))
            return jnp.concatenate([middle, tail], axis=1)

        for power in range(depth + 1):
            reach = depth - power
            now = work.at[power % 2]
            old = work.at[1 - power % 2]
            for y in range(-reach, rows + reach):
                if power == 0:
                    value = raw(y)
                else:
                    x = old[y + REACH]
                    value = pltpu.roll(x, 1, 1) + pltpu.roll(x, width - 1, 1)
                    value = value + (old[y + REACH - 1] + old[y + REACH + 1])
                    value = value * keep[0 if y < 0 else 1 if y < rows else 2]
                now[y + REACH] = value
                if 0 <= y < rows:
                    first = power * group + which * half_group
                    right[y, first : first + planes, :] = value[:, :lanes]

    powers(0)
    powers(1)

    size = 2 * planes
    for y in range(rows):
        value = jnp.dot(left[...], right[y], precision=lax.Precision.HIGHEST, preferred_element_type=jnp.float32)
        for i in range(nz - 1):
            outgoing[i, y] = value[i * size : (i + 1) * size]
            copy_if(True, outgoing.at[i, y], incoming.at[i, y],
                    part_ss.at[i, y], part_rs.at[i, y], at(lax.rem(gz + 1 + i, nz), gy, gx))
        mine[y] = value[(nz - 1) * size :]
    for y in range(rows):
        value = mine[y]
        for i in range(nz - 1):
            arrive_if(True, incoming.at[i, y], part_ss.at[i, y], part_rs.at[i, y])
            value = value + incoming[i, y]
        for tile in range(tiles):
            part = value[:, tile * 128 : (tile + 1) * 128]
            spots = pl.ds(tile * rows + y, planes, stride=tiles * rows)
            out_u[spots, :] = part[:planes]
            out_r[spots, :] = part[planes:]
    for cond, copy in pending:
        @pl.when(cond)
        def _(copy=copy):
            copy.wait_send()


def solution(mesh):
    sizes = tuple(mesh.shape[name] for name in ("gz", "gy", "gx"))
    nz = sizes[0]

    def on_device(right_side, start_field, layer_material, stiffness, line_factors):
        dims = right_side.shape
        layers, comps, rows, lanes = dims
        planes = layers * comps
        deep = nz * layers
        half_group = -(-planes // 32) * 32
        depth = POWERS * 2 * half_group
        packed = -(-2 * rows * SLOT // 128) * 128
        f32 = jnp.float32
        vmem = pl.BlockSpec(memory_space=pltpu.VMEM)
        smem = pl.BlockSpec(memory_space=pltpu.SMEM)
        dma = pltpu.SemaphoreType.DMA
        others = max(nz - 1, 1)
        symbol = pltpu.VMEM((deep * comps, 8, 128), f32)
        scratch = [pltpu.SMEM((nz, layers), jnp.int32)]
        scratch += [pltpu.VMEM((rows, planes, lanes), f32)] * 2
        scratch += [pltpu.VMEM((n, planes, lanes), f32) for n in (REACH, REACH - 1, REACH, REACH - 1)]
        scratch += [
            pltpu.VMEM((2, planes, packed), f32),
            pltpu.VMEM((2, 3, planes, packed), f32),
            pltpu.VMEM((2, rows + 2 * REACH, planes, lanes + 128), f32),
            pltpu.VMEM((3, planes, lanes + 128), f32),
        ]
        scratch += [symbol] * 6
        scratch += [
            pltpu.VMEM((nz * 2 * planes * 8, 128), f32),
            pltpu.VMEM((nz * 2 * planes, depth), f32),
            pltpu.VMEM((rows, depth, lanes), f32),
            pltpu.VMEM((rows, 2 * planes, lanes), f32),
            pltpu.VMEM((others, rows, 2 * planes, lanes), f32),
            pltpu.VMEM((others, rows, 2 * planes, lanes), f32),
        ]
        scratch += [dma((nz,))] * 2 + [dma((2, 2))] * 2 + [dma((2, 3))] * 2 + [dma((others, rows))] * 2
        tiled = (layers, comps, rows, lanes // 128, 128)

        def flatten(x):
            return x.reshape(tiled).transpose(0, 1, 3, 2, 4).reshape(-1, 128)

        def unflatten(x):
            split = x.reshape(layers, comps, lanes // 128, rows, 128)
            return split.transpose(0, 1, 3, 2, 4).reshape(dims)

        out = jax.ShapeDtypeStruct((planes * rows * lanes // 128, 128), f32)
        outs = pl.pallas_call(
            functools.partial(kernel, sizes, dims),
            out_shape=(out, out),
            in_specs=[smem, smem, smem, vmem, vmem],
            out_specs=(vmem, vmem),
            scratch_shapes=scratch,
            compiler_params=pltpu.CompilerParams(
                collective_id=0, has_side_effects=True, vmem_limit_bytes=VMEM_LIMIT),
        )(layer_material, stiffness.transpose(1, 2, 3, 0), line_factors.transpose(1, 2, 3, 0),
          flatten(right_side), flatten(start_field))
        return tuple(unflatten(o) for o in outs)

    return jax.shard_map(
        on_device,
        mesh=mesh,
        in_specs=(P("gz", None, "gy", "gx"), P("gz", None, "gy", "gx"), P("gz"), P(), P()),
        out_specs=(P("gz", None, "gy", "gx"), P("gz", None, "gy", "gx")),
        check_vma=False,
    )


VMEM_LIMIT = 40 * 1024 * 1024
```

time: 41.7 us -> 33.6 us (0.81)
  the two profiles are of different devices: /device:TPU:1 before, /device:TPU:0 now
where the time goes in v1:
time: 33.6 us; the launch traced here: 33.4 us
  Pallas kernels  27.4 us (82%)
  local copies, waits for them, and re-layouts  5.3 us (16%)
  between operations  0.65 us (2%)
    pallas_call x1, Pallas kernels, on_device(): pl.pallas_call(functools.partial(kernel, sizes, dims), out_shape=(out, ou...  27.4 us
    unnamed x12, local copies, waits for them, and re-layouts  5.3 us

profile of v1, /device:TPU:0, one launch (start us, length us, event | category | flops | bytes accessed | tf_op | source)
XLA Modules:
  0.0 33.4 jit_solution(3233059105077390884)
XLA Ops:
  0.6 0.0 copy-start.4
  0.6 0.6 %copy-done.4 = s32[8]{0:T(128)S(1)} copy-done((s32[8]{0:T(128)S(1)}, s32[8]{0:T(128)}, u32[]{:S(2)}) %copy-start.4) | copy-done | bytes 56
  1.3 0.0 copy-start
  1.3 0.9 %copy-done = f32[8,3,8,256]{3,2,1,0:T(8,128)S(1)} copy-done((f32[8,3,8,256]{3,2,1,0:T(8,128)S(1)}, f32[8,3,8,256]{3,2,1,0:T(8,128)}, u32[]{:S(2)}) %copy-start) | copy-done | bytes 196632
  2.2 0.0 copy-start.1
  2.2 0.9 %copy-done.1 = f32[8,3,8,256]{3,2,1,0:T(8,128)S(1)} copy-done((f32[8,3,8,256]{3,2,1,0:T(8,128)S(1)}, f32[8,3,8,256]{3,2,1,0:T(8,128)}, u32[]{:S(2)}) %copy-start.1) | copy-done | bytes 196632
  3.1 0.0 copy-start.2
  3.1 0.7 %copy-done.2 = f32[8,3,3,3]{0,3,2,1:T(4,128)S(1)} copy-done((f32[8,3,3,3]{0,3,2,1:T(4,128)S(1)}, f32[8,3,3,3]{0,3,2,1:T(4,128)}, u32[]{:S(2)}) %copy-start.2) | copy-done | bytes 888
  3.9 0.0 copy-start.3
  3.9 0.7 %copy-done.3 = f32[8,3,3,3]{0,3,2,1:T(4,128)S(1)} copy-done((f32[8,3,3,3]{0,3,2,1:T(4,128)S(1)}, f32[8,3,3,3]{0,3,2,1:T(4,128)}, u32[]{:S(2)}) %copy-start.3) | copy-done | bytes 888
  4.6 27.4 %shard_map.68 = (f32[384,128]{1,0:T(8,128)S(1)}, f32[384,128]{1,0:T(8,128)S(1)}) custom-call(s32[8]{0:T(128)S(1)} %copy-done.4, f32[3,3,3,8]{3,2,1,0:T(4,128)S(1)} %bitcast.26, f32[3,3,3,8]{3,2,1,0:T(4,128)S(1)} %bitcast.27, f32[384,128]{1,0:T(8,128)S(1)} %bitcast.24, f32[384,128]{1,0:T(8,128)S(1)} %bitcast.25), custom_call_target="tpu_custom_call" | custom-call | tf_op jit(solution)/shard_map/pallas_call | solution.py:369
  32.0 0.7 %copy.9 = f32[8,3,8,256]{3,2,1,0:T(8,128)} copy(f32[8,3,8,256]{3,2,1,0:T(8,128)S(1)} %bitcast.23) | data formatting | bytes 393216
  32.7 0.7 %copy.10 = f32[8,3,8,256]{3,2,1,0:T(8,128)} copy(f32[8,3,8,256]{3,2,1,0:T(8,128)S(1)} %bitcast.22) | data formatting | bytes 393216
Async XLA Ops:
  0.6 0.7 %copy-start.4 = (s32[8]{0:T(128)S(1)}, s32[8]{0:T(128)}, u32[]{:S(2)}) copy-start(s32[8]{0:T(128)} %material.1) | copy-start | bytes 100
  1.3 0.9 %copy-start = (f32[8,3,8,256]{3,2,1,0:T(8,128)S(1)}, f32[8,3,8,256]{3,2,1,0:T(8,128)}, u32[]{:S(2)}) copy-start(f32[8,3,8,256]{3,2,1,0:T(8,128)} %param.5) | copy-start | bytes 589828
  2.2 0.9 %copy-start.1 = (f32[8,3,8,256]{3,2,1,0:T(8,128)S(1)}, f32[8,3,8,256]{3,2,1,0:T(8,128)}, u32[]{:S(2)}) copy-start(f32[8,3,8,256]{3,2,1,0:T(8,128)} %param.6) | copy-start | bytes 589828
  3.1 0.7 %copy-start.2 = (f32[8,3,3,3]{0,3,2,1:T(4,128)S(1)}, f32[8,3,3,3]{0,3,2,1:T(4,128)}, u32[]{:S(2)}) copy-start(f32[8,3,3,3]{0,3,2,1:T(4,128)} %param.8) | copy-start | bytes 2596
  3.9 0.7 %copy-start.3 = (f32[8,3,3,3]{0,3,2,1:T(4,128)S(1)}, f32[8,3,3,3]{0,3,2,1:T(4,128)}, u32[]{:S(2)}) copy-start(f32[8,3,3,3]{0,3,2,1:T(4,128)} %param.9) | copy-start | bytes 2596

commit v2 on v1

--- a/solution.py
+++ b/solution.py
@@ -22,8 +22,9 @@
 
 
 def kernel(
-    sizes, dims, material, sten, fac, load, start, out_u, out_r,
-    mats, own_u, own_b, prev_u, prev_b, next_u, next_b, edge_out, edge_in, work, keep,
+    sizes, dims, material_hbm, sten_hbm, fac_hbm, load_hbm, start_hbm, out_u, out_r,
+    material, sten, fac, load, start, coef, in_sem,
+    mats, own_u, own_b, prev_u, prev_b, next_u, next_b, edge_out, edge_in, work_u, work_b, keep,
     sym_u, sym_b, sym_r, sym_y, sym_e, sym_c, maps, left, right, mine, outgoing, incoming,
     mat_ss, mat_rs, row_ss, row_rs, edge_ss, edge_rs, part_ss, part_rs,
 ):
@@ -34,9 +35,17 @@
     width = lanes + 128
     gz, gy, gx = (lax.axis_index(name) for name in ("gz", "gy", "gx"))
     three = range(comps)
-    group = right.shape[1] // POWERS
-    half_group = group // 2
+    half_group = -(-planes // 32) * 32
+    depth = POWERS * half_group
     pending = []
+    fetches = [
+        pltpu.make_async_copy(src, dst, in_sem.at[i])
+        for i, (src, dst) in enumerate((
+            (start_hbm, start), (load_hbm, load), (sten_hbm, sten), (fac_hbm, fac), (material_hbm, material),
+        ))
+    ]
+    for fetch in fetches:
+        fetch.start()
 
     def at(z, y, x):
         return {"gz": z, "gy": y, "gx": x}
@@ -47,19 +56,26 @@
             device_id=target, device_id_type=MESH,
         )
 
-        @pl.when(cond)
-        def _():
+        if cond is True:
             copy.start()
+        else:
+            @pl.when(cond)
+            def _():
+                copy.start()
 
         pending.append((cond, copy))
 
     def arrive_if(cond, ref, ss, rs):
-        @pl.when(cond)
-        def _():
-            pltpu.make_async_remote_copy(
-                src_ref=ref, dst_ref=ref, send_sem=ss, recv_sem=rs,
-                device_id=at(gz, gy, gx), device_id_type=MESH,
-            ).wait_recv()
+        copy = pltpu.make_async_remote_copy(
+            src_ref=ref, dst_ref=ref, send_sem=ss, recv_sem=rs,
+            device_id=at(gz, gy, gx), device_id_type=MESH,
+        )
+        if cond is True:
+            copy.wait_recv()
+        else:
+            @pl.when(cond)
+            def _():
+                copy.wait_recv()
 
     has_prev_y, has_next_y = gy > 0, gy < ny - 1
     has_prev_x, has_next_x = gx > 0, gx < nx - 1
@@ -78,7 +94,8 @@
             pl.semaphore_signal(barrier, inc=1, device_id=target, device_id_type=MESH)
 
     tiles = lanes // 128
-    for own, given in ((own_u, start), (own_b, load)):
+    for own, given, fetch in ((own_u, start, fetches[0]), (own_b, load, fetches[1])):
+        fetch.wait()
         for y in range(rows):
             for tile in range(tiles):
                 own[y, :, tile * 128 : (tile + 1) * 128] = given[pl.ds(tile * rows + y, planes, stride=tiles * rows), :]
@@ -103,6 +120,7 @@
                     packed = jnp.where(inside, piece, packed)
             edge_out[side, :, tile * 128 : (tile + 1) * 128] = packed
 
+    fetches[4].wait()
     pl.semaphore_wait(barrier, total([cond.astype(jnp.int32) for cond, _ in peers]))
 
     for j in range(nz):
@@ -114,14 +132,38 @@
                     edge_ss.at[1 - side, 1 - step_y], edge_rs.at[1 - side, 1 - step_y],
                     at(gz, gy + step_y, gx + step_x))
     strips = ((own_u, prev_u, next_u, REACH), (own_b, prev_b, next_b, REACH - 1))
-    for which, (own, prev, after, depth) in enumerate(strips):
-        copy_if(has_next_y, own.at[rows - depth : rows], prev,
-                row_ss.at[which, 0], row_rs.at[which, 0], at(gz, gy + 1, gx))
-        copy_if(has_prev_y, own.at[0:depth], after,
-                row_ss.at[which, 1], row_rs.at[which, 1], at(gz, gy - 1, gx))
+    stages = rows // 2
+
+    def known(which, stage):
+        return max(strips[which][3] - stages + 1 + stage, 0)
+
+    def strip(which, stage):
+        own, prev, after, reach = strips[which]
+        first = known(which, stage - 1) if stage else 0
+        last = known(which, stage)
+        return ((own.at[rows - last : rows - first], prev.at[reach - last : reach - first]),
+                (own.at[first:last], after.at[first:last]))
+
+    for stage in range(stages):
+        for which in range(2):
+            (out_up, in_up), (out_down, in_down) = strip(which, stage)
+            copy_if(has_next_y, out_up, in_up,
+                    row_ss.at[which, stage, 0], row_rs.at[which, stage, 0], at(gz, gy + 1, gx))
+            copy_if(has_prev_y, out_down, in_down,
+                    row_ss.at[which, stage, 1], row_rs.at[which, stage, 1], at(gz, gy - 1, gx))
 
     for layer in range(layers):
         mats[gz, layer] = material[layer]
+    blocks = 3 * comps * comps
+    for fetch in fetches[2:4]:
+        fetch.wait()
+    for first, table in ((0, sten), (blocks, fac)):
+        for which in range(3):
+            for i in three:
+                for j in three:
+                    for mat_id in range(coef.shape[0]):
+                        spot = first + (which * comps + i) * comps + j
+                        coef[mat_id, spot] = jnp.full((8, 128), table[which, i, j, mat_id], jnp.float32)
     for cond, refs in ((has_prev_y, (prev_u, prev_b)), (has_next_y, (next_u, next_b))):
         @pl.when(jnp.logical_not(cond))
         def _(refs=refs):
@@ -140,17 +182,9 @@
     keep[0] = inner * has_prev_y.astype(jnp.float32)
     keep[1] = inner
     keep[2] = inner * has_next_y.astype(jnp.float32)
-    for y in range(rows):
-        for power in range(POWERS):
-            for part in range(2):
-                if power == REACH and part == 1:
-                    low = 0
-                else:
-                    low = planes
-                if low < half_group:
-                    first = power * group + part * half_group + low
-                    stop = power * group + (part + 1) * half_group
-                    right[y, first:stop, :] = jnp.zeros((stop - first, lanes), jnp.float32)
+    for part in range(3):
+        for y in range(rows):
+            right[part, y, 2 * depth - half_group :, :] = jnp.zeros((half_group, lanes), jnp.bfloat16)
 
     sub = lax.broadcasted_iota(jnp.int32, (8, 128), 0)
     lane = lax.broadcasted_iota(jnp.int32, (8, 128), 1)
@@ -159,10 +193,8 @@
     def block(table, level, layer, which):
         z = layer * (2 if level else 1)
         mat_id = mats[z // layers, z % layers]
-        values = [[table[which, i, j, mat_id] for j in three] for i in three]
-        if level and table is sten and which == 2:
-            values = [[0.25 * v for v in line] for line in values]
-        return values
+        first = which * comps * comps + (blocks if table is fac else 0)
+        return [[coef[mat_id, first + i * comps + j] for j in three] for i in three]
 
     def times(mat, vec):
         return [total([mat[i][j] * vec[j] for j in three]) for i in three]
@@ -188,7 +220,7 @@
                 near.append(field[(layer - 1) * comps + c])
             if layer < count - 1:
                 near.append(field[(layer + 1) * comps + c])
-            vert.append(total(near))
+            vert.append(0.25 * total(near) if level else total(near))
         a = times(block(sten, level, layer, 0), here)
         b = times(block(sten, level, layer, 1), side)
         d = times(block(sten, level, layer, 2), vert)
@@ -238,72 +270,101 @@
             maps[(first + c) * 8 : (first + c + 1) * 8, :] = sym_u[z * comps + c]
             spot = first + planes + c
             maps[spot * 8 : (spot + 1) * 8, :] = value[c]
+    def thirds(x):
+        high = x.astype(jnp.bfloat16)
+        rest = x - high.astype(jnp.float32)
+        middle = rest.astype(jnp.bfloat16)
+        return high, middle, (rest - middle.astype(jnp.float32)).astype(jnp.bfloat16)
+
+    size = 2 * planes
+    count = nz * size
+    map_lane = lax.broadcasted_iota(jnp.int32, (size, 128), 1)
     for i in range(nz):
         target = lax.rem(gz + 1 + i, nz)
-        for pair in range(POWERS * group // 128):
-            tile = None
-            for part in range(128 // group):
-                power = pair * (128 // group) + part
-                value = maps[pl.ds(target * 2 * planes * 8 + power, 2 * planes, stride=8), :]
-                if part:
-                    value = pltpu.roll(value, part * group, 1)
-                tile = value if tile is None else tile + value
-            left[i * 2 * planes : (i + 1) * 2 * planes, pair * 128 : (pair + 1) * 128] = tile
+        lines = [maps[pl.ds(target * size * 8 + power, size, stride=8), :] for power in range(POWERS)]
+        for which in range(2):
+            base = which * half_group
+            inside = jnp.logical_and(map_lane >= base, map_lane < base + half_group)
+            each = 128 // half_group
+            for tile in range(POWERS // each):
+                value = jnp.zeros((size, 128), jnp.float32)
+                for part in range(each):
+                    piece = jnp.where(inside, lines[tile * each + part], 0.0)
+                    shift = (part * half_group - base) % 128
+                    value = value + (pltpu.roll(piece, shift, 1) if shift else piece)
+                first = which * depth + tile * 128
+                for part, third in enumerate(thirds(value)):
+                    left[part * count + i * size : part * count + (i + 1) * size, first : first + 128] = third
 
     for step_y, cond_y in sides_y:
         for side, (step_x, cond_x) in enumerate(sides_x):
             arrive_if(jnp.logical_and(cond_y, cond_x), edge_in.at[side, 1 + step_y],
                       edge_ss.at[side, 1 + step_y], edge_rs.at[side, 1 + step_y])
 
-    def powers(which):
-        own, prev, after, depth = strips[which]
-        arrive_if(has_prev_y, prev, row_ss.at[which, 0], row_rs.at[which, 0])
-        arrive_if(has_next_y, after, row_ss.at[which, 1], row_rs.at[which, 1])
-
-        def raw(y):
-            if y < 0:
-                middle, step_y, line = prev[depth + y], -1, rows + y
-            elif y < rows:
-                middle, step_y, line = own[y], 0, y
-            else:
-                middle, step_y, line = after[y - rows], 1, y - rows
-            base, spot = place(which * rows + line)
-            west = pltpu.roll(edge_in[0, 1 + step_y, :, base : base + 128], (128 - SLOT - spot) % 128, 1)
-            east = edge_in[1, 1 + step_y, :, base : base + 128]
-            if spot:
-                east = pltpu.roll(east, 128 - spot, 1)
-            tail = jnp.where(tile_lane < SLOT, east, jnp.where(tile_lane >= 128 - SLOT, west, 0.0))
-            return jnp.concatenate([middle, tail], axis=1)
-
-        for power in range(depth + 1):
-            reach = depth - power
-            now = work.at[power % 2]
-            old = work.at[1 - power % 2]
-            for y in range(-reach, rows + reach):
+    def raw(which, y):
+        own, prev, after, reach = strips[which]
+        if y < 0:
+            middle, step_y, line = prev[reach + y], -1, rows + y
+        elif y < rows:
+            middle, step_y, line = own[y], 0, y
+        else:
+            middle, step_y, line = after[y - rows], 1, y - rows
+        base, spot = place(which * rows + line)
+        west = pltpu.roll(edge_in[0, 1 + step_y, :, base : base + 128], (128 - SLOT - spot) % 128, 1)
+        east = edge_in[1, 1 + step_y, :, base : base + 128]
+        if spot:
+            east = pltpu.roll(east, 128 - spot, 1)
+        tail = jnp.where(tile_lane < SLOT, east, jnp.where(tile_lane >= 128 - SLOT, west, 0.0))
+        return jnp.concatenate([middle, tail], axis=1)
+
+    padding = jnp.zeros((half_group - planes, lanes), jnp.float32)
+    done = set()
+
+    def extend(which, known_rows):
+        work, reach = (work_u, work_b)[which], strips[which][3]
+        for power in range(reach + 1):
+            for y in range(power - known_rows, rows + known_rows - power):
+                if (which, power, y) in done:
+                    continue
+                done.add((which, power, y))
                 if power == 0:
-                    value = raw(y)
+                    value = raw(which, y)
                 else:
-                    x = old[y + REACH]
+                    x = work[power - 1, y + reach]
                     value = pltpu.roll(x, 1, 1) + pltpu.roll(x, width - 1, 1)
-                    value = value + (old[y + REACH - 1] + old[y + REACH + 1])
+                    value = value + (work[power - 1, y + reach - 1] + work[power - 1, y + reach + 1])
                     value = value * keep[0 if y < 0 else 1 if y < rows else 2]
-                now[y + REACH] = value
+                if power < reach:
+                    work[power, y + reach] = value
                 if 0 <= y < rows:
-                    first = power * group + which * half_group
-                    right[y, first : first + planes, :] = value[:, :lanes]
-
-    powers(0)
-    powers(1)
-
-    size = 2 * planes
-    for y in range(rows):
-        value = jnp.dot(left[...], right[y], precision=lax.Precision.HIGHEST, preferred_element_type=jnp.float32)
-        for i in range(nz - 1):
-            outgoing[i, y] = value[i * size : (i + 1) * size]
-            copy_if(True, outgoing.at[i, y], incoming.at[i, y],
-                    part_ss.at[i, y], part_rs.at[i, y], at(lax.rem(gz + 1 + i, nz), gy, gx))
-        mine[y] = value[(nz - 1) * size :]
-    for y in range(rows):
+                    first = which * depth + power * half_group
+                    cell = value[:, :lanes]
+                    if half_group > planes:
+                        cell = jnp.concatenate([cell, padding], axis=0)
+                    for part, third in enumerate(thirds(cell)):
+                        right[part, y, first : first + half_group, :] = third
+
+    for which in range(2):
+        extend(which, 0)
+    for stage in range(stages):
+        for which in range(2):
+            (_, in_up), (_, in_down) = strip(which, stage)
+            arrive_if(has_prev_y, in_up, row_ss.at[which, stage, 0], row_rs.at[which, stage, 0])
+            arrive_if(has_next_y, in_down, row_ss.at[which, stage, 1], row_rs.at[which, stage, 1])
+        for which in range(2):
+            extend(which, known(which, stage))
+        for y in (stages - 1 - stage, stages + stage):
+            pieces = []
+            for part in (2, 1, 0):
+                product = jnp.dot(left[: (3 - part) * count], right[part, y], preferred_element_type=jnp.float32)
+                pieces += [product[k * count : (k + 1) * count] for k in reversed(range(3 - part))]
+            value = total(pieces)
+            for i in range(nz - 1):
+                outgoing[i, y] = value[i * size : (i + 1) * size]
+                copy_if(True, outgoing.at[i, y], incoming.at[i, y],
+                        part_ss.at[i, y], part_rs.at[i, y], at(lax.rem(gz + 1 + i, nz), gy, gx))
+            mine[y] = value[(nz - 1) * size :]
+    for y in [y for stage in range(stages) for y in (stages - 1 - stage, stages + stage)]:
         value = mine[y]
         for i in range(nz - 1):
             arrive_if(True, incoming.at[i, y], part_ss.at[i, y], part_rs.at[i, y])
@@ -314,9 +375,12 @@
             out_u[spots, :] = part[:planes]
             out_r[spots, :] = part[planes:]
     for cond, copy in pending:
-        @pl.when(cond)
-        def _(copy=copy):
+        if cond is True:
             copy.wait_send()
+        else:
+            @pl.when(cond)
+            def _(copy=copy):
+                copy.wait_send()
 
 
 def solution(mesh):
@@ -333,29 +397,35 @@
         packed = -(-2 * rows * SLOT // 128) * 128
         f32 = jnp.float32
         vmem = pl.BlockSpec(memory_space=pltpu.VMEM)
-        smem = pl.BlockSpec(memory_space=pltpu.SMEM)
         dma = pltpu.SemaphoreType.DMA
         others = max(nz - 1, 1)
         symbol = pltpu.VMEM((deep * comps, 8, 128), f32)
-        scratch = [pltpu.SMEM((nz, layers), jnp.int32)]
+        tables = (3, comps, comps, stiffness.shape[0])
+        flat = (planes * rows * lanes // 128, 128)
+        scratch = [pltpu.SMEM((layers,), jnp.int32)]
+        scratch += [pltpu.SMEM(tables, f32)] * 2
+        scratch += [pltpu.VMEM(flat, f32)] * 2
+        scratch += [pltpu.VMEM((tables[3], 2 * 3 * comps * comps, 8, 128), f32), dma((5,))]
+        scratch += [pltpu.SMEM((nz, layers), jnp.int32)]
         scratch += [pltpu.VMEM((rows, planes, lanes), f32)] * 2
         scratch += [pltpu.VMEM((n, planes, lanes), f32) for n in (REACH, REACH - 1, REACH, REACH - 1)]
         scratch += [
             pltpu.VMEM((2, planes, packed), f32),
             pltpu.VMEM((2, 3, planes, packed), f32),
-            pltpu.VMEM((2, rows + 2 * REACH, planes, lanes + 128), f32),
+            pltpu.VMEM((REACH, rows + 2 * REACH, planes, lanes + 128), f32),
+            pltpu.VMEM((REACH - 1, rows + 2 * REACH - 2, planes, lanes + 128), f32),
             pltpu.VMEM((3, planes, lanes + 128), f32),
         ]
         scratch += [symbol] * 6
         scratch += [
             pltpu.VMEM((nz * 2 * planes * 8, 128), f32),
-            pltpu.VMEM((nz * 2 * planes, depth), f32),
-            pltpu.VMEM((rows, depth, lanes), f32),
+            pltpu.VMEM((3 * nz * 2 * planes, depth), jnp.bfloat16),
+            pltpu.VMEM((3, rows, depth, lanes), jnp.bfloat16),
             pltpu.VMEM((rows, 2 * planes, lanes), f32),
             pltpu.VMEM((others, rows, 2 * planes, lanes), f32),
             pltpu.VMEM((others, rows, 2 * planes, lanes), f32),
         ]
-        scratch += [dma((nz,))] * 2 + [dma((2, 2))] * 2 + [dma((2, 3))] * 2 + [dma((others, rows))] * 2
+        scratch += [dma((nz,))] * 2 + [dma((2, rows // 2, 2))] * 2 + [dma((2, 3))] * 2 + [dma((others, rows))] * 2
         tiled = (layers, comps, rows, lanes // 128, 128)
 
         def flatten(x):
@@ -365,17 +435,19 @@
             split = x.reshape(layers, comps, lanes // 128, rows, 128)
             return split.transpose(0, 1, 3, 2, 4).reshape(dims)
 
-        out = jax.ShapeDtypeStruct((planes * rows * lanes // 128, 128), f32)
+        out = jax.ShapeDtypeStruct(flat, f32)
+        given = (layer_material, stiffness.transpose(1, 2, 3, 0), line_factors.transpose(1, 2, 3, 0),
+                 flatten(right_side), flatten(start_field))
+        given = [pltpu.with_memory_space_constraint(x, pltpu.HBM) for x in given]
         outs = pl.pallas_call(
             functools.partial(kernel, sizes, dims),
             out_shape=(out, out),
-            in_specs=[smem, smem, smem, vmem, vmem],
+            in_specs=[pl.BlockSpec(memory_space=pltpu.HBM)] * 5,
             out_specs=(vmem, vmem),
             scratch_shapes=scratch,
             compiler_params=pltpu.CompilerParams(
                 collective_id=0, has_side_effects=True, vmem_limit_bytes=VMEM_LIMIT),
-        )(layer_material, stiffness.transpose(1, 2, 3, 0), line_factors.transpose(1, 2, 3, 0),
-          flatten(right_side), flatten(start_field))
+        )(*given)
         return tuple(unflatten(o) for o in outs)
 
     return jax.shard_map(

time: 33.6 us -> 25.4 us (0.76)
  the two profiles are of different devices: /device:TPU:0 before, /device:TPU:1 now
where the time goes in v2:
time: 25.4 us; the launch traced here: 25 us
  Pallas kernels  23 us (91%)
  local copies, waits for them, and re-layouts  1.36 us (5%)
  between operations  0.64 us (3%)
    pallas_call x1, Pallas kernels, on_device(): pl.pallas_call(functools.partial(kernel, sizes, dims), out_shape=(out, ou...  23 us
    unnamed x2, local copies, waits for them, and re-layouts  1.36 us

profile of v2, /device:TPU:1, one launch (start us, length us, event | category | flops | bytes accessed | tf_op | source)
XLA Modules:
  0.0 25.0 jit_solution(5563742036530197920)
XLA Ops:
  0.6 23.0 %shard_map.68 = (f32[384,128]{1,0:T(8,128)S(1)}, f32[384,128]{1,0:T(8,128)S(1)}) custom-call(s32[8]{0:T(128)} %material_hbm.1, f32[3,3,3,8]{3,2,1,0:T(4,128)} %bitcast.26, f32[3,3,3,8]{3,2,1,0:T(4,128)} %bitcast.27, f32[384,128]{1,0:T(8,128)} %bitcast.24, f32[384,128]{1,0:T(8,128)} %bitcast.25), custom_call_target="tpu_custom_call" | custom-call | tf_op jit(solution)/shard_map/pallas_call | solution.py:442
  23.7 0.7 %copy.9 = f32[8,3,8,256]{3,2,1,0:T(8,128)} copy(f32[8,3,8,256]{3,2,1,0:T(8,128)S(1)} %bitcast.23) | data formatting | bytes 393216
  24.3 0.7 %copy.10 = f32[8,3,8,256]{3,2,1,0:T(8,128)} copy(f32[8,3,8,256]{3,2,1,0:T(8,128)S(1)} %bitcast.22) | data formatting | bytes 393216

commit v3 on v2

--- a/solution.py
+++ b/solution.py
@@ -26,7 +26,7 @@
     material, sten, fac, load, start, coef, in_sem,
     mats, own_u, own_b, prev_u, prev_b, next_u, next_b, edge_out, edge_in, work_u, work_b, keep,
     sym_u, sym_b, sym_r, sym_y, sym_e, sym_c, maps, left, right, mine, outgoing, incoming,
-    mat_ss, mat_rs, row_ss, row_rs, edge_ss, edge_rs, part_ss, part_rs,
+    mat_ss, mat_rs, row_ss, row_rs, edge_ss, edge_rs, pass_ss, pass_rs, part_ss, part_rs,
 ):
     nz, ny, nx = sizes
     layers, comps, rows, lanes = dims
@@ -79,15 +79,13 @@
 
     has_prev_y, has_next_y = gy > 0, gy < ny - 1
     has_prev_x, has_next_x = gx > 0, gx < nx - 1
-    sides_y = ((-1, has_prev_y), (0, True), (1, has_next_y))
+    sides_y = ((-1, has_prev_y), (1, has_next_y))
     sides_x = ((-1, has_prev_x), (1, has_next_x))
 
     barrier = pltpu.get_barrier_semaphore()
     peers = [(gz != j, at(j, gy, gx)) for j in range(nz)]
-    peers += [(cond, at(gz, gy + step, gx)) for step, cond in sides_y if step]
-    for step_y, cond_y in sides_y:
-        for step_x, cond_x in sides_x:
-            peers.append((jnp.logical_and(cond_y, cond_x), at(gz, gy + step_y, gx + step_x)))
+    peers += [(cond, at(gz, gy + step, gx)) for step, cond in sides_y]
+    peers += [(cond, at(gz, gy, gx + step)) for step, cond in sides_x]
     for cond, target in peers:
         @pl.when(cond)
         def _(target=target):
@@ -125,32 +123,39 @@
 
     for j in range(nz):
         copy_if(gz != j, material, mats.at[gz], mat_ss.at[j], mat_rs.at[gz], at(j, gy, gx))
-    for step_y, cond_y in sides_y:
-        for side, (step_x, cond_x) in enumerate(sides_x):
-            slot = edge_in.at[1 - side, 1 - step_y]
-            copy_if(jnp.logical_and(cond_y, cond_x), edge_out.at[side], slot,
-                    edge_ss.at[1 - side, 1 - step_y], edge_rs.at[1 - side, 1 - step_y],
-                    at(gz, gy + step_y, gx + step_x))
     strips = ((own_u, prev_u, next_u, REACH), (own_b, prev_b, next_b, REACH - 1))
     stages = rows // 2
-
-    def known(which, stage):
-        return max(strips[which][3] - stages + 1 + stage, 0)
-
-    def strip(which, stage):
+    bounds = []
+    for which, shared in ((0, 2), (1, 1)):
+        reach = strips[which][3]
+        enough = max(reach - stages + 1, 0)
+        bounds.append(sorted({0, enough}) + list(range(enough + 1, reach + 1)))
+    spans = [list(zip(b[:-1], b[1:])) for b in bounds]
+    opening = [len([1 for _, last in spans[which] if last <= max(strips[which][3] - stages + 1, 0)]) for which in range(2)]
+
+    def strip(which, step):
         own, prev, after, reach = strips[which]
-        first = known(which, stage - 1) if stage else 0
-        last = known(which, stage)
+        first, last = spans[which][step]
         return ((own.at[rows - last : rows - first], prev.at[reach - last : reach - first]),
                 (own.at[first:last], after.at[first:last]))
 
-    for stage in range(stages):
-        for which in range(2):
-            (out_up, in_up), (out_down, in_down) = strip(which, stage)
-            copy_if(has_next_y, out_up, in_up,
-                    row_ss.at[which, stage, 0], row_rs.at[which, stage, 0], at(gz, gy + 1, gx))
-            copy_if(has_prev_y, out_down, in_down,
-                    row_ss.at[which, stage, 1], row_rs.at[which, stage, 1], at(gz, gy - 1, gx))
+    def send_rows(which, step):
+        (out_up, in_up), (out_down, in_down) = strip(which, step)
+        copy_if(has_next_y, out_up, in_up,
+                row_ss.at[which, step, 0], row_rs.at[which, step, 0], at(gz, gy + 1, gx))
+        copy_if(has_prev_y, out_down, in_down,
+                row_ss.at[which, step, 1], row_rs.at[which, step, 1], at(gz, gy - 1, gx))
+
+    early = [(0, step) for step in range(opening[0])]
+    later = [(1, step) for step in range(opening[1])]
+    for more in range(max(len(spans[0]) - opening[0], len(spans[1]) - opening[1])):
+        later += [(w, opening[w] + more) for w in range(2) if opening[w] + more < len(spans[w])]
+    for side, (step_x, cond_x) in enumerate(sides_x):
+        copy_if(cond_x, edge_out.at[side], edge_in.at[1, 1 - side],
+                edge_ss.at[1 - side], edge_rs.at[1 - side], at(gz, gy, gx + step_x))
+
+    for which, step in early:
+        send_rows(which, step)
 
     for layer in range(layers):
         mats[gz, layer] = material[layer]
@@ -169,11 +174,20 @@
         def _(refs=refs):
             for ref in refs:
                 ref[...] = jnp.zeros_like(ref)
-    for step_y, cond_y in sides_y:
-        for side, (step_x, cond_x) in enumerate(sides_x):
-            @pl.when(jnp.logical_not(jnp.logical_and(cond_y, cond_x)))
-            def _(side=side, step_y=step_y):
-                edge_in[side, 1 + step_y] = jnp.zeros_like(edge_in[side, 1 + step_y])
+    for spot, (step_y, cond_y) in enumerate(sides_y):
+        @pl.when(jnp.logical_not(cond_y))
+        def _(spot=spot):
+            edge_in[2 * spot] = jnp.zeros_like(edge_in[2 * spot])
+    for side, (step_x, cond_x) in enumerate(sides_x):
+        @pl.when(jnp.logical_not(cond_x))
+        def _(side=side):
+            edge_in[1, side] = jnp.zeros_like(edge_in[1, side])
+    for side, (step_x, cond_x) in enumerate(sides_x):
+        arrive_if(cond_x, edge_in.at[1, side], edge_ss.at[side], edge_rs.at[side])
+    copy_if(has_next_y, edge_in.at[1], edge_in.at[0], pass_ss.at[0], pass_rs.at[0], at(gz, gy + 1, gx))
+    copy_if(has_prev_y, edge_in.at[1], edge_in.at[2], pass_ss.at[1], pass_rs.at[1], at(gz, gy - 1, gx))
+    for which, step in later:
+        send_rows(which, step)
     wide_lane = lax.broadcasted_iota(jnp.int32, (planes, width), 1)
     inner = (wide_lane < lanes).astype(jnp.float32)
     inner = inner + jnp.where(
@@ -185,6 +199,9 @@
     for part in range(3):
         for y in range(rows):
             right[part, y, 2 * depth - half_group :, :] = jnp.zeros((half_group, lanes), jnp.bfloat16)
+
+    for j in range(nz):
+        arrive_if(gz != j, mats.at[j], mat_ss.at[j], mat_rs.at[j])
 
     sub = lax.broadcasted_iota(jnp.int32, (8, 128), 0)
     lane = lax.broadcasted_iota(jnp.int32, (8, 128), 1)
@@ -245,8 +262,6 @@
                 field[spot] = now[c] if fresh else field[spot] + now[c]
             back = now
 
-    for j in range(nz):
-        arrive_if(gz != j, mats.at[j], mat_ss.at[j], mat_rs.at[j])
     for sweep in range(SWEEPS):
         line_solve(0, lambda layer: residual(0, sym_u, sym_b, deep, layer), sym_u, deep, False)
     for k in range(deep // 2):
@@ -296,11 +311,6 @@
                 for part, third in enumerate(thirds(value)):
                     left[part * count + i * size : part * count + (i + 1) * size, first : first + 128] = third
 
-    for step_y, cond_y in sides_y:
-        for side, (step_x, cond_x) in enumerate(sides_x):
-            arrive_if(jnp.logical_and(cond_y, cond_x), edge_in.at[side, 1 + step_y],
-                      edge_ss.at[side, 1 + step_y], edge_rs.at[side, 1 + step_y])
-
     def raw(which, y):
         own, prev, after, reach = strips[which]
         if y < 0:
@@ -310,8 +320,8 @@
         else:
             middle, step_y, line = after[y - rows], 1, y - rows
         base, spot = place(which * rows + line)
-        west = pltpu.roll(edge_in[0, 1 + step_y, :, base : base + 128], (128 - SLOT - spot) % 128, 1)
-        east = edge_in[1, 1 + step_y, :, base : base + 128]
+        west = pltpu.roll(edge_in[1 + step_y, 0, :, base : base + 128], (128 - SLOT - spot) % 128, 1)
+        east = edge_in[1 + step_y, 1, :, base : base + 128]
         if spot:
             east = pltpu.roll(east, 128 - spot, 1)
         tail = jnp.where(tile_lane < SLOT, east, jnp.where(tile_lane >= 128 - SLOT, west, 0.0))
@@ -344,15 +354,22 @@
                     for part, third in enumerate(thirds(cell)):
                         right[part, y, first : first + half_group, :] = third
 
+    def take(which, step):
+        (_, in_up), (_, in_down) = strip(which, step)
+        arrive_if(has_prev_y, in_up, row_ss.at[which, step, 0], row_rs.at[which, step, 0])
+        arrive_if(has_next_y, in_down, row_ss.at[which, step, 1], row_rs.at[which, step, 1])
+        extend(which, spans[which][step][1])
+
     for which in range(2):
         extend(which, 0)
+    for spot, (step_y, cond_y) in enumerate(sides_y):
+        arrive_if(cond_y, edge_in.at[2 * spot], pass_ss.at[spot], pass_rs.at[spot])
     for stage in range(stages):
         for which in range(2):
-            (_, in_up), (_, in_down) = strip(which, stage)
-            arrive_if(has_prev_y, in_up, row_ss.at[which, stage, 0], row_rs.at[which, stage, 0])
-            arrive_if(has_next_y, in_down, row_ss.at[which, stage, 1], row_rs.at[which, stage, 1])
-        for which in range(2):
-            extend(which, known(which, stage))
+            first = opening[which] + stage - 1 if stage else 0
+            for step in range(first, opening[which] + stage):
+                if step < len(spans[which]):
+                    take(which, step)
         for y in (stages - 1 - stage, stages + stage):
             pieces = []
             for part in (2, 1, 0):
@@ -383,6 +400,14 @@
                 copy.wait_send()
 
 
+def put(from_u, from_r, to_u, to_r, sem):
+    copies = [pltpu.make_async_copy(src, dst, sem.at[i]) for i, (src, dst) in enumerate(((from_u, to_u), (from_r, to_r)))]
+    for copy in copies:
+        copy.start()
+    for copy in copies:
+        copy.wait()
+
+
 def solution(mesh):
     sizes = tuple(mesh.shape[name] for name in ("gz", "gy", "gx"))
     nz = sizes[0]
@@ -411,7 +436,7 @@
         scratch += [pltpu.VMEM((n, planes, lanes), f32) for n in (REACH, REACH - 1, REACH, REACH - 1)]
         scratch += [
             pltpu.VMEM((2, planes, packed), f32),
-            pltpu.VMEM((2, 3, planes, packed), f32),
+            pltpu.VMEM((3, 2, planes, packed), f32),
             pltpu.VMEM((REACH, rows + 2 * REACH, planes, lanes + 128), f32),
             pltpu.VMEM((REACH - 1, rows + 2 * REACH - 2, planes, lanes + 128), f32),
             pltpu.VMEM((3, planes, lanes + 128), f32),
@@ -425,7 +450,7 @@
             pltpu.VMEM((others, rows, 2 * planes, lanes), f32),
             pltpu.VMEM((others, rows, 2 * planes, lanes), f32),
         ]
-        scratch += [dma((nz,))] * 2 + [dma((2, rows // 2, 2))] * 2 + [dma((2, 3))] * 2 + [dma((others, rows))] * 2
+        scratch += [dma((nz,))] * 2 + [dma((2, REACH, 2))] * 2 + [dma((2,))] * 4 + [dma((others, rows))] * 2
         tiled = (layers, comps, rows, lanes // 128, 128)
 
         def flatten(x):
@@ -448,6 +473,14 @@
             compiler_params=pltpu.CompilerParams(
                 collective_id=0, has_side_effects=True, vmem_limit_bytes=VMEM_LIMIT),
         )(*given)
+        outs = pl.pallas_call(
+            put,
+            out_shape=(out, out),
+            in_specs=[vmem, vmem],
+            out_specs=(pl.BlockSpec(memory_space=pltpu.HBM),) * 2,
+            scratch_shapes=[dma((2,))],
+            compiler_params=pltpu.CompilerParams(vmem_limit_bytes=4 * 1024 * 1024),
+        )(*outs)
         return tuple(unflatten(o) for o in outs)
 
     return jax.shard_map(

time: 25.4 us -> 23.5 us (0.925)
  local copies, waits for them, and re-layouts: 1.36 us -> 0 us
  Pallas kernels: 23 us -> 22.7 us
    unnamed x2 -> x0, local copies, waits for them, and re-layouts: 1.36 us -> none
    pallas_call x1, Pallas kernels: 23 us -> 21.9 us  [on_device(): pl.pallas_call(functools.partial(kernel, sizes, dims), out_shape=(out, ou...]
    pallas_call x0 -> x1, Pallas kernels: none -> 0.76 us  [on_device(): pl.pallas_call(put, out_shape=(out, out), in_specs=[vmem, vmem], out_spec...]
where the time goes in v3:
time: 23.5 us; the launch traced here: 23.3 us
  Pallas kernels  22.7 us (97%)
  between operations  0.64 us (3%)
    pallas_call x1, Pallas kernels, on_device(): pl.pallas_call(functools.partial(kernel, sizes, dims), out_shape=(out, ou...  21.9 us
    pallas_call x1, Pallas kernels, on_device(): pl.pallas_call(put, out_shape=(out, out), in_specs=[vmem, vmem], out_spec...  0.76 us

profile of v3, /device:TPU:1, one launch (start us, length us, event | category | flops | bytes accessed | tf_op | source)
XLA Modules:
  0.0 23.3 jit_solution(13423650478096321022)
XLA Ops:
  0.6 21.9 %shard_map.68 = (f32[384,128]{1,0:T(8,128)S(1)}, f32[384,128]{1,0:T(8,128)S(1)}) custom-call(s32[8]{0:T(128)} %material_hbm.1, f32[3,3,3,8]{3,2,1,0:T(4,128)} %bitcast.24, f32[3,3,3,8]{3,2,1,0:T(4,128)} %bitcast.25, f32[384,128]{1,0:T(8,128)} %bitcast.22, f32[384,128]{1,0:T(8,128)} %bitcast.23), custom_call_target="tpu_custom_call" | custom-call | tf_op jit(solution)/shard_map/pallas_call | solution.py:467
  22.5 0.8 %shard_map.69 = (f32[384,128]{1,0:T(8,128)}, f32[384,128]{1,0:T(8,128)}) custom-call(f32[384,128]{1,0:T(8,128)S(1)} %get-tuple-element.6.from_u, f32[384,128]{1,0:T(8,128)S(1)} %get-tuple-element.7.from_r), custom_call_target="tpu_custom_call" | custom-call | tf_op jit(solution)/shard_map/pallas_call | solution.py:476

commit v4 on v3

--- a/solution.py
+++ b/solution.py
@@ -25,8 +25,8 @@
     sizes, dims, material_hbm, sten_hbm, fac_hbm, load_hbm, start_hbm, out_u, out_r,
     material, sten, fac, load, start, coef, in_sem,
     mats, own_u, own_b, prev_u, prev_b, next_u, next_b, edge_out, edge_in, work_u, work_b, keep,
-    sym_u, sym_b, sym_r, sym_y, sym_e, sym_c, maps, left, right, mine, outgoing, incoming,
-    mat_ss, mat_rs, row_ss, row_rs, edge_ss, edge_rs, pass_ss, pass_rs, part_ss, part_rs,
+    sym_u, sym_b, sym_r, sym_y, sym_e, sym_c, maps, left, right, mine, outgoing, incoming, rim_out, rim_in, side_out, side_in,
+    mat_ss, mat_rs, row_ss, row_rs, edge_ss, edge_rs, pass_ss, pass_rs, part_ss, part_rs, rim_ss, rim_rs, side_ss, side_rs,
 ):
     nz, ny, nx = sizes
     layers, comps, rows, lanes = dims
@@ -364,6 +364,15 @@
         extend(which, 0)
     for spot, (step_y, cond_y) in enumerate(sides_y):
         arrive_if(cond_y, edge_in.at[2 * spot], pass_ss.at[spot], pass_rs.at[spot])
+    rim_id = lax.broadcasted_iota(jnp.int32, (8, lanes), 0)
+    rim_low, rim_high = rim_id < comps, rim_id >= 8 - comps
+    columns = [jnp.zeros((planes, 128), jnp.float32)] * (nz - 1)
+
+    def side_tile(field, y):
+        first = jnp.where(tile_lane == 2 * y, pltpu.roll(field[:, :128], 2 * y, 1), 0.0)
+        last = jnp.where(tile_lane == 2 * y + 1, pltpu.roll(field[:, lanes - 128 :], (2 * y + 2) % 128, 1), 0.0)
+        return first + last
+
     for stage in range(stages):
         for which in range(2):
             first = opening[which] + stage - 1 if stage else 0
@@ -377,20 +386,100 @@
                 pieces += [product[k * count : (k + 1) * count] for k in reversed(range(3 - part))]
             value = total(pieces)
             for i in range(nz - 1):
-                outgoing[i, y] = value[i * size : (i + 1) * size]
-                copy_if(True, outgoing.at[i, y], incoming.at[i, y],
-                        part_ss.at[i, y], part_rs.at[i, y], at(lax.rem(gz + 1 + i, nz), gy, gx))
+                target = at(lax.rem(gz + 1 + i, nz), gy, gx)
+                share = value[i * size : (i + 1) * size]
+                whole = y in (0, rows - 1)
+                outgoing[i, y] = share
+                amount = size if whole else planes
+                copy_if(True, outgoing.at[i, y, 0:amount], incoming.at[i, y, 0:amount],
+                        part_ss.at[i, y], part_rs.at[i, y], target)
+                if whole:
+                    continue
+                ends = share[planes : planes + 8], share[size - 8 : size]
+                rim_out[i, y] = jnp.where(rim_low, ends[0], ends[1])
+                copy_if(True, rim_out.at[i, y], rim_in.at[i, y], rim_ss.at[i, y], rim_rs.at[i, y], target)
+                columns[i] = columns[i] + side_tile(share[planes:], y)
+                if stage == stages - 2 and y == stages + stage:
+                    side_out[i] = columns[i]
+                    copy_if(True, side_out.at[i], side_in.at[i], side_ss.at[i], side_rs.at[i], target)
             mine[y] = value[(nz - 1) * size :]
+    rest_id = lax.broadcasted_iota(jnp.int32, (planes, 128), 0)
     for y in [y for stage in range(stages) for y in (stages - 1 - stage, stages + stage)]:
         value = mine[y]
+        whole = y in (0, rows - 1)
+        solved, rest = value[:planes], value[planes:]
         for i in range(nz - 1):
-            arrive_if(True, incoming.at[i, y], part_ss.at[i, y], part_rs.at[i, y])
-            value = value + incoming[i, y]
+            amount = size if whole else planes
+            arrive_if(True, incoming.at[i, y, 0:amount], part_ss.at[i, y], part_rs.at[i, y])
+            solved = solved + incoming[i, y, 0:planes]
+            if whole:
+                rest = rest + incoming[i, y, planes:size]
         for tile in range(tiles):
-            part = value[:, tile * 128 : (tile + 1) * 128]
             spots = pl.ds(tile * rows + y, planes, stride=tiles * rows)
-            out_u[spots, :] = part[:planes]
-            out_r[spots, :] = part[planes:]
+            out_u[spots, :] = solved[:, tile * 128 : (tile + 1) * 128]
+            if whole:
+                out_r[spots, :] = rest[:, tile * 128 : (tile + 1) * 128]
+        if y == 1:
+            for i in range(nz - 1):
+                arrive_if(True, side_in.at[i], side_ss.at[i], side_rs.at[i])
+        if y == rows - 2:
+            sides = total([side_in[i] for i in range(nz - 1)]) if nz > 1 else jnp.zeros((planes, 128), jnp.float32)
+            for line in range(1, rows - 1):
+                rest = mine[line][planes:]
+                ends = jnp.zeros((8, lanes), jnp.float32)
+                for i in range(nz - 1):
+                    arrive_if(True, rim_in.at[i, line], rim_ss.at[i, line], rim_rs.at[i, line])
+                    ends = ends + rim_in[i, line]
+                ends = [jnp.where(rim_low, ends, 0.0), jnp.where(rim_high, ends, 0.0)]
+                cut = [rest[:8] + ends[0], rest[8 : planes - 8], rest[planes - 8 :] + ends[1]]
+                rest = jnp.concatenate(cut, axis=0)
+                inner_side = jnp.logical_and(rest_id >= comps, rest_id < planes - comps)
+                for tile in range(tiles):
+                    part = rest[:, tile * 128 : (tile + 1) * 128]
+                    if tile == 0:
+                        add = pltpu.roll(sides, 128 - 2 * line, 1)
+                        part = part + jnp.where(jnp.logical_and(inner_side, tile_lane == 0), add, 0.0)
+                    if tile == tiles - 1:
+                        add = pltpu.roll(sides, 126 - 2 * line, 1)
+                        part = part + jnp.where(jnp.logical_and(inner_side, tile_lane == 127), add, 0.0)
+                    out_r[pl.ds(tile * rows + line, planes, stride=tiles * rows), :] = part
+
+    row_id = lax.broadcasted_iota(jnp.int32, (rows, 128), 0)
+    lane_id = lax.broadcasted_iota(jnp.int32, (rows, 128), 1)
+    row_rim = jnp.logical_or(row_id == 0, row_id == rows - 1)
+
+    def solution_tile(layer, c, tile):
+        first = ((layer * comps + c) * tiles + tile) * rows
+        return pl.ds(first, rows)
+
+    def shares(layer, first):
+        mat_id = mats[gz, layer]
+        return [[coef[mat_id, first + i * comps + j] for j in three] for i in three]
+
+    for layer in range(1, layers - 1):
+        mat = [shares(layer, which * comps * comps) for which in range(3)]
+        for tile in range(tiles):
+            here, side, vert = [], [], []
+            for c in three:
+                x = out_u[solution_tile(layer, c, tile), :]
+                west = out_u[solution_tile(layer, c, tile - 1), :] if tile else x
+                east = out_u[solution_tile(layer, c, tile + 1), :] if tile < tiles - 1 else x
+                beside = jnp.where(lane_id == 127, west, x), jnp.where(lane_id == 0, east, x)
+                around = pltpu.roll(beside[0], 1, 1) + pltpu.roll(beside[1], 127, 1)
+                here.append(x)
+                side.append(around + (pltpu.roll(x, 1, 0) + pltpu.roll(x, rows - 1, 0)))
+                vert.append(out_u[solution_tile(layer - 1, c, tile), :] + out_u[solution_tile(layer + 1, c, tile), :])
+            a, b, d = (times(mat[which], vec) for which, vec in enumerate((here, side, vert)))
+            rim = row_rim
+            if tile == 0:
+                rim = jnp.logical_or(rim, lane_id == 0)
+            if tile == tiles - 1:
+                rim = jnp.logical_or(rim, lane_id == 127)
+            for c in three:
+                spot = solution_tile(layer, c, tile)
+                first = ((layer * comps + c) * tiles + tile) * rows
+                value = load[first : first + rows, :] - (a[c] - b[c] - d[c])
+                out_r[spot, :] = jnp.where(rim, out_r[spot, :], value)
     for cond, copy in pending:
         if cond is True:
             copy.wait_send()
@@ -450,7 +539,8 @@
             pltpu.VMEM((others, rows, 2 * planes, lanes), f32),
             pltpu.VMEM((others, rows, 2 * planes, lanes), f32),
         ]
-        scratch += [dma((nz,))] * 2 + [dma((2, REACH, 2))] * 2 + [dma((2,))] * 4 + [dma((others, rows))] * 2
+        scratch += [pltpu.VMEM((others, rows, 8, lanes), f32)] * 2 + [pltpu.VMEM((others, planes, 128), f32)] * 2
+        scratch += [dma((nz,))] * 2 + [dma((2, REACH, 2))] * 2 + [dma((2,))] * 4 + [dma((others, rows))] * 4 + [dma((others,))] * 2
         tiled = (layers, comps, rows, lanes // 128, 128)
 
         def flatten(x):

time: 23.5 us -> 22.3 us (0.949)
  Pallas kernels: 22.7 us -> 21.5 us
    pallas_call x1, Pallas kernels: 21.9 us -> 20.8 us  [on_device(): pl.pallas_call(functools.partial(kernel, sizes, dims), out_shape=(out, ou...]
where the time goes in v4:
time: 22.3 us; the launch traced here: 22.2 us
  Pallas kernels  21.5 us (96%)
  between operations  0.64 us (3%)
    pallas_call x1, Pallas kernels, on_device(): pl.pallas_call(functools.partial(kernel, sizes, dims), out_shape=(out, ou...  20.8 us
    pallas_call x1, Pallas kernels, on_device(): pl.pallas_call(put, out_shape=(out, out), in_specs=[vmem, vmem], out_spec...  0.76 us

profile of v4, /device:TPU:1, one launch (start us, length us, event | category | flops | bytes accessed | tf_op | source)
XLA Modules:
  0.0 22.2 jit_solution(9227391725665237184)
XLA Ops:
  0.6 20.8 %shard_map.68 = (f32[384,128]{1,0:T(8,128)S(1)}, f32[384,128]{1,0:T(8,128)S(1)}) custom-call(s32[8]{0:T(128)} %material_hbm.1, f32[3,3,3,8]{3,2,1,0:T(4,128)} %bitcast.24, f32[3,3,3,8]{3,2,1,0:T(4,128)} %bitcast.25, f32[384,128]{1,0:T(8,128)} %bitcast.22, f32[384,128]{1,0:T(8,128)} %bitcast.23), custom_call_target="tpu_custom_call" | custom-call | tf_op jit(solution)/shard_map/pallas_call | solution.py:557
  21.4 0.8 %shard_map.69 = (f32[384,128]{1,0:T(8,128)}, f32[384,128]{1,0:T(8,128)}) custom-call(f32[384,128]{1,0:T(8,128)S(1)} %get-tuple-element.6.from_u, f32[384,128]{1,0:T(8,128)S(1)} %get-tuple-element.7.from_r), custom_call_target="tpu_custom_call" | custom-call | tf_op jit(solution)/shard_map/pallas_call | solution.py:566

commit v5 on v4

--- a/solution.py
+++ b/solution.py
@@ -395,15 +395,27 @@
                         part_ss.at[i, y], part_rs.at[i, y], target)
                 if whole:
                     continue
-                ends = share[planes : planes + 8], share[size - 8 : size]
-                rim_out[i, y] = jnp.where(rim_low, ends[0], ends[1])
-                copy_if(True, rim_out.at[i, y], rim_in.at[i, y], rim_ss.at[i, y], rim_rs.at[i, y], target)
+                low, high = share[planes : planes + 8], share[size - 8 : size]
+                upper = y >= stages
+                if nz == 2:
+                    ends = jnp.where(gz == 1, pltpu.roll(high, comps, 0), low)
+                    if upper:
+                        ends = jnp.where(rim_id < 4, held, pltpu.roll(ends, 4, 0))
+                    held = ends
+                else:
+                    ends = jnp.where(rim_low, low, high)
+                if nz > 2 or upper:
+                    spot = (i, stage, int(upper) if nz > 2 else 0)
+                    rim_out[spot] = ends
+                    copy_if(True, rim_out.at[spot], rim_in.at[spot], rim_ss.at[spot], rim_rs.at[spot], target)
                 columns[i] = columns[i] + side_tile(share[planes:], y)
                 if stage == stages - 2 and y == stages + stage:
                     side_out[i] = columns[i]
                     copy_if(True, side_out.at[i], side_in.at[i], side_ss.at[i], side_rs.at[i], target)
             mine[y] = value[(nz - 1) * size :]
     rest_id = lax.broadcasted_iota(jnp.int32, (planes, 128), 0)
+    taken = set()
+    open_low, open_high = (gz == 0, gz == 1) if nz == 2 else (False, False)
     for y in [y for stage in range(stages) for y in (stages - 1 - stage, stages + stage)]:
         value = mine[y]
         whole = y in (0, rows - 1)
@@ -426,14 +438,25 @@
             sides = total([side_in[i] for i in range(nz - 1)]) if nz > 1 else jnp.zeros((planes, 128), jnp.float32)
             for line in range(1, rows - 1):
                 rest = mine[line][planes:]
-                ends = jnp.zeros((8, lanes), jnp.float32)
+                ends = [jnp.zeros((8, lanes), jnp.float32)] * 2
+                upper = line >= stages
+                stage = line - stages if upper else stages - 1 - line
                 for i in range(nz - 1):
-                    arrive_if(True, rim_in.at[i, line], rim_ss.at[i, line], rim_rs.at[i, line])
-                    ends = ends + rim_in[i, line]
-                ends = [jnp.where(rim_low, ends, 0.0), jnp.where(rim_high, ends, 0.0)]
+                    spot = (i, stage, int(upper) if nz > 2 else 0)
+                    if spot not in taken:
+                        taken.add(spot)
+                        arrive_if(True, rim_in.at[spot], rim_ss.at[spot], rim_rs.at[spot])
+                    given = rim_in[spot]
+                    if nz == 2:
+                        given = pltpu.roll(given, 4, 0) if upper else given
+                        ends = [jnp.where(jnp.logical_and(rim_low, gz == 1), given, 0.0),
+                                jnp.where(jnp.logical_and(rim_high, gz == 0), pltpu.roll(given, 8 - comps, 0), 0.0)]
+                    else:
+                        ends = [ends[0] + jnp.where(rim_low, given, 0.0), ends[1] + jnp.where(rim_high, given, 0.0)]
                 cut = [rest[:8] + ends[0], rest[8 : planes - 8], rest[planes - 8 :] + ends[1]]
                 rest = jnp.concatenate(cut, axis=0)
-                inner_side = jnp.logical_and(rest_id >= comps, rest_id < planes - comps)
+                inner_side = jnp.logical_and(
+                    jnp.logical_or(rest_id >= comps, open_low), jnp.logical_or(rest_id < planes - comps, open_high))
                 for tile in range(tiles):
                     part = rest[:, tile * 128 : (tile + 1) * 128]
                     if tile == 0:
@@ -456,7 +479,7 @@
         mat_id = mats[gz, layer]
         return [[coef[mat_id, first + i * comps + j] for j in three] for i in three]
 
-    for layer in range(1, layers - 1):
+    for layer in range(layers) if nz == 2 else range(1, layers - 1):
         mat = [shares(layer, which * comps * comps) for which in range(3)]
         for tile in range(tiles):
             here, side, vert = [], [], []
@@ -468,9 +491,12 @@
                 around = pltpu.roll(beside[0], 1, 1) + pltpu.roll(beside[1], 127, 1)
                 here.append(x)
                 side.append(around + (pltpu.roll(x, 1, 0) + pltpu.roll(x, rows - 1, 0)))
-                vert.append(out_u[solution_tile(layer - 1, c, tile), :] + out_u[solution_tile(layer + 1, c, tile), :])
+                near = [out_u[solution_tile(z, c, tile), :] for z in (layer - 1, layer + 1) if 0 <= z < layers]
+                vert.append(total(near))
             a, b, d = (times(mat[which], vec) for which, vec in enumerate((here, side, vert)))
             rim = row_rim
+            if layer in (0, layers - 1):
+                rim = jnp.logical_or(rim, jnp.logical_not(open_high if layer else open_low))
             if tile == 0:
                 rim = jnp.logical_or(rim, lane_id == 0)
             if tile == tiles - 1:
@@ -539,8 +565,8 @@
             pltpu.VMEM((others, rows, 2 * planes, lanes), f32),
             pltpu.VMEM((others, rows, 2 * planes, lanes), f32),
         ]
-        scratch += [pltpu.VMEM((others, rows, 8, lanes), f32)] * 2 + [pltpu.VMEM((others, planes, 128), f32)] * 2
-        scratch += [dma((nz,))] * 2 + [dma((2, REACH, 2))] * 2 + [dma((2,))] * 4 + [dma((others, rows))] * 4 + [dma((others,))] * 2
+        scratch += [pltpu.VMEM((others, rows // 2, 2, 8, lanes), f32)] * 2 + [pltpu.VMEM((others, planes, 128), f32)] * 2
+        scratch += [dma((nz,))] * 2 + [dma((2, REACH, 2))] * 2 + [dma((2,))] * 4 + [dma((others, rows))] * 2 + [dma((others, rows // 2, 2))] * 2 + [dma((others,))] * 2
         tiled = (layers, comps, rows, lanes // 128, 128)
 
         def flatten(x):

time: 22.3 us -> 22.2 us (level)
  no operation moved by 1% of the time
where the time goes in v5:
time: 22.2 us; the launch traced here: 22 us
  Pallas kernels  21.4 us (96%)
  between operations  0.64 us (3%)
    pallas_call x1, Pallas kernels, on_device(): pl.pallas_call(functools.partial(kernel, sizes, dims), out_shape=(out, ou...  20.6 us
    pallas_call x1, Pallas kernels, on_device(): pl.pallas_call(put, out_shape=(out, out), in_specs=[vmem, vmem], out_spec...  0.76 us

profile of v5, /device:TPU:1, one launch (start us, length us, event | category | flops | bytes accessed | tf_op | source)
XLA Modules:
  0.0 22.0 jit_solution(6848580931254616542)
XLA Ops:
  0.6 20.6 %shard_map.68 = (f32[384,128]{1,0:T(8,128)S(1)}, f32[384,128]{1,0:T(8,128)S(1)}) custom-call(s32[8]{0:T(128)} %material_hbm.1, f32[3,3,3,8]{3,2,1,0:T(4,128)} %bitcast.24, f32[3,3,3,8]{3,2,1,0:T(4,128)} %bitcast.25, f32[384,128]{1,0:T(8,128)} %bitcast.22, f32[384,128]{1,0:T(8,128)} %bitcast.23), custom_call_target="tpu_custom_call" | custom-call | tf_op jit(solution)/shard_map/pallas_call | solution.py:583
  21.3 0.8 %shard_map.69 = (f32[384,128]{1,0:T(8,128)}, f32[384,128]{1,0:T(8,128)}) custom-call(f32[384,128]{1,0:T(8,128)S(1)} %get-tuple-element.6.from_u, f32[384,128]{1,0:T(8,128)S(1)} %get-tuple-element.7.from_r), custom_call_target="tpu_custom_call" | custom-call | tf_op jit(solution)/shard_map/pallas_call | solution.py:592

commit v6 on v5

--- a/solution.py
+++ b/solution.py
@@ -330,6 +330,13 @@
     padding = jnp.zeros((half_group - planes, lanes), jnp.float32)
     done = set()
 
+    def put_powers(which, power, y, cell):
+        first = which * depth + power * half_group
+        if half_group > planes:
+            cell = jnp.concatenate([cell, padding], axis=0)
+        for part, third in enumerate(thirds(cell)):
+            right[part, y, first : first + half_group, :] = third
+
     def extend(which, known_rows):
         work, reach = (work_u, work_b)[which], strips[which][3]
         for power in range(reach + 1):
@@ -341,18 +348,22 @@
                     value = raw(which, y)
                 else:
                     x = work[power - 1, y + reach]
+                    if power == reach:
+                        parts = [x[:, k : k + 128] for k in range(0, width, 128)]
+                        west = [jnp.where(tile_lane == 127, parts[k - 1], parts[k]) for k in range(tiles)]
+                        east = [jnp.where(tile_lane == 0, parts[k + 1], parts[k]) for k in range(tiles)]
+                        near = [pltpu.roll(a, 1, 1) + pltpu.roll(b, 127, 1) for a, b in zip(west, east)]
+                        cross = work[power - 1, y + reach - 1, :, :lanes] + work[power - 1, y + reach + 1, :, :lanes]
+                        value = jnp.concatenate(near, axis=1) + cross
+                        put_powers(which, power, y, value)
+                        continue
                     value = pltpu.roll(x, 1, 1) + pltpu.roll(x, width - 1, 1)
                     value = value + (work[power - 1, y + reach - 1] + work[power - 1, y + reach + 1])
                     value = value * keep[0 if y < 0 else 1 if y < rows else 2]
                 if power < reach:
                     work[power, y + reach] = value
                 if 0 <= y < rows:
-                    first = which * depth + power * half_group
-                    cell = value[:, :lanes]
-                    if half_group > planes:
-                        cell = jnp.concatenate([cell, padding], axis=0)
-                    for part, third in enumerate(thirds(cell)):
-                        right[part, y, first : first + half_group, :] = third
+                    put_powers(which, power, y, value[:, :lanes])
 
     def take(which, step):
         (_, in_up), (_, in_down) = strip(which, step)

time: 22.2 us -> 22.1 us (level)
  no operation moved by 1% of the time
where the time goes in v6:
time: 22.1 us; the launch traced here: 22 us
  Pallas kernels  21.3 us (96%)
  between operations  0.64 us (3%)
    pallas_call x1, Pallas kernels, on_device(): pl.pallas_call(functools.partial(kernel, sizes, dims), out_shape=(out, ou...  20.6 us
    pallas_call x1, Pallas kernels, on_device(): pl.pallas_call(put, out_shape=(out, out), in_specs=[vmem, vmem], out_spec...  0.76 us

profile of v6, /device:TPU:1, one launch (start us, length us, event | category | flops | bytes accessed | tf_op | source)
XLA Modules:
  0.0 22.0 jit_solution(6527722497483741447)
XLA Ops:
  0.6 20.6 %shard_map.68 = (f32[384,128]{1,0:T(8,128)S(1)}, f32[384,128]{1,0:T(8,128)S(1)}) custom-call(s32[8]{0:T(128)} %material_hbm.1, f32[3,3,3,8]{3,2,1,0:T(4,128)} %bitcast.24, f32[3,3,3,8]{3,2,1,0:T(4,128)} %bitcast.25, f32[384,128]{1,0:T(8,128)} %bitcast.22, f32[384,128]{1,0:T(8,128)} %bitcast.23), custom_call_target="tpu_custom_call" | custom-call | tf_op jit(solution)/shard_map/pallas_call | solution.py:594
  21.2 0.8 %shard_map.69 = (f32[384,128]{1,0:T(8,128)}, f32[384,128]{1,0:T(8,128)}) custom-call(f32[384,128]{1,0:T(8,128)S(1)} %get-tuple-element.6.from_u, f32[384,128]{1,0:T(8,128)S(1)} %get-tuple-element.7.from_r), custom_call_target="tpu_custom_call" | custom-call | tf_op jit(solution)/shard_map/pallas_call | solution.py:603
